TPU v7x, 128 devices: a whole 4x4x4 slice. The times are simulated.
128 devices in a mesh: rows: 4 (over z_hi, core), cols: 32 (over x, z_lo, y).
Axes of the slice: x: 4, y: 4, z: 4 (z_hi: 2, z_lo: 2; z = z_hi * 2 + z_lo), core: 2. Of those that a mesh axis runs over, the one named last changes fastest.
Arguments:
- tokens: bfloat16 [2048, 6144], P('rows', 'cols'), may hold values from -6 to 6
- cotangent: bfloat16 [2048, 16384], P('rows', 'cols'), may hold values from -0.049804688 to 0.049804688
- weight: bfloat16 [6144, 16384], P(None, 'cols'), may hold values from -6 to 6
- momentum: float32 [128, 768, 1024], P(('rows', 'cols')), may hold values from -40 to 40
Outputs:
- new_weight: bfloat16 [6144, 16384], P(None, 'cols')
- input_grad: bfloat16 [2048, 6144], P('rows', 'cols')
- new_momentum: float32 [128, 768, 1024], P(('rows', 'cols'))
- update: float32 [128, 768, 1024], P(('rows', 'cols'))
All inputs are finite; a program needn't handle non-finite values.
Results may differ from a plain program's by a relative error of at most 0.012.
Values may be sent and summed in bfloat16 or wider, within the bound.
A program may use at most 128 MiB of HBM per device.

v0:
```python
import jax
import jax.numpy as jnp
from jax import lax
from jax.sharding import Mesh
from jax.sharding import PartitionSpec as P

NS_STEPS = 2
COLS = ("cols_0", "cols_1", "cols_2")
ROWS_COLS = ("rows", "cols_0", "cols_1", "cols_2")


coef_a = 3.4445
coef_b = -4.775
coef_c = 2.0315
beta_mom = 0.95
step_rate = 0.25


def reduced_to_own(pieces, axes, sequence):
    inside = pieces.shape[1:]
    pieces = pieces.reshape(*(lax.axis_size(a) for a in axes), *inside)
    pieces = jnp.moveaxis(pieces, sequence, range(len(axes))).reshape(-1, *inside)
    for k in sequence:
        pieces = lax.psum_scatter(pieces, axes[k], scatter_dimension=0, tiled=True)
    return pieces[0]


def cut_along(x, dim, count):
    before, after = (x.shape[:dim], x.shape[dim + 1 :])
    return jnp.moveaxis(x.reshape(*before, count, -1, *after), dim, 0)


def summed_rows(x, axes, sequence, dim):
    count = lax.axis_size(axes)
    return reduced_to_own(cut_along(x, dim, count), axes, sequence)


def partner(x, axis, bit):
    return lax.ppermute(x, axis, [(i, i ^ 1 << bit) for i in range(lax.axis_size(axis))])


def orthogonalize(matrix):
    norm_value = jnp.sqrt(jnp.sum(matrix * matrix))
    current = (matrix / (norm_value + 1e-07)).astype(jnp.bfloat16)
    for index in range(NS_STEPS):
        square = jnp.dot(current, current.T, preferred_element_type=jnp.float32).astype(
            jnp.bfloat16
        )
        poly = (
            coef_b * square.astype(jnp.float32)
            + coef_c * jnp.dot(square, square, preferred_element_type=jnp.float32)
        ).astype(jnp.bfloat16)
        current = (
            coef_a * current.astype(jnp.float32)
            + jnp.dot(poly, current, preferred_element_type=jnp.float32)
        ).astype(jnp.bfloat16)
    return current


def body(tokens, cotangent, weight, momentum):
    half_bit = lax.axis_index(COLS) % 2
    other_bit = 1 - half_bit
    groups = lax.axis_size("rows")
    partial_value = lax.dot_general(
        lax.all_gather(tokens, COLS, axis=1, tiled=True),
        cotangent,
        (((0,), (0,)), ((), ())),
        preferred_element_type=jnp.float32,
    )
    terms = lax.dot_general(
        cotangent, weight, (((1,), (1,)), ((), ())), preferred_element_type=jnp.float32
    )
    input_grad = summed_rows(terms, COLS, (0, 2, 1), 1).astype(jnp.bfloat16)
    d_rows, f_cols = partial_value.shape
    block_rows = d_rows // (2 * groups)
    summed = lax.psum_scatter(partial_value, "rows", scatter_dimension=0, tiled=True)
    split = summed.reshape(2, block_rows, f_cols)
    mine = lax.dynamic_index_in_dim(split, half_bit, 0, keepdims=False)
    theirs = lax.dynamic_index_in_dim(split, other_bit, 0, keepdims=False)
    received = partner(theirs, COLS, 0)
    joined = jnp.where(
        half_bit == 0, jnp.concatenate([mine, received], 1), jnp.concatenate([received, mine], 1)
    )
    grad_block = joined[None]
    new_momentum = beta_mom * momentum + grad_block
    block_cols = new_momentum.shape[2]
    scale_value = float(max(block_rows, block_cols)) ** 0.5
    update = scale_value * orthogonalize(new_momentum[0]).astype(jnp.float32)
    sent = update.astype(jnp.bfloat16)
    col_split = sent.reshape(block_rows, 2, f_cols)
    mine = lax.dynamic_index_in_dim(col_split, half_bit, 1, keepdims=False)
    theirs = lax.dynamic_index_in_dim(col_split, other_bit, 1, keepdims=False)
    received = partner(theirs, COLS, 0)
    stacked = jnp.where(
        half_bit == 0, jnp.concatenate([mine, received], 0), jnp.concatenate([received, mine], 0)
    )
    placed = lax.all_gather(stacked, "rows", axis=0, tiled=True)
    new_weight = (weight.astype(jnp.float32) - step_rate * placed.astype(jnp.float32)).astype(
        jnp.bfloat16
    )
    return (new_weight, input_grad, new_momentum, update[None])


def solution(mesh):
    torus = Mesh(
        mesh.devices.reshape(mesh.shape["rows"], 4, 2, 4), ("rows", "cols_0", "cols_1", "cols_2")
    )
    in_specs = (P("rows", COLS), P("rows", COLS), P(None, COLS), P(ROWS_COLS, None, None))
    out_specs = (P(None, COLS), P("rows", COLS), P(ROWS_COLS, None, None), P(ROWS_COLS, None, None))
    return jax.shard_map(body, mesh=torus, in_specs=in_specs, out_specs=out_specs, check_vma=False)
```

profile of v0, /device:TPU:0, one launch (start us, length us, event | category | flops | bytes accessed | tf_op | source)
XLA Modules:
  0.0 556.7 jit_solution(7268899705757204786)
XLA Ops:
  8.0 0.0 copy-start
  8.0 0.0 all-gather.3.cloned.1.call-start
  8.1 0.7 all-gather.3.cloned.1.call-update
  8.7 0.0 reduce-scatter.7.cloned.1.call-start
  8.8 0.2 copy-done
  9.0 9.2 %fusion.15 = f32[512,6144]{0,1:T(8,128)} fusion(bf16[512,512]{1,0:T(8,128)(2,1)S(1)} %copy-done, bf16[6144,512]{1,0:T(8,128)(2,1)} %param.6), kind=kOutput, calls=%fused_computation.30 | convolution fusion | flops 3221225472 | bytes 19398656 | tf_op jit(solution)/shard_map/dot_general | solution.py:70
  18.3 11.6 %copy.15 = f32[4,4,2,512,192]{3,4,2,1,0:T(8,128)} copy(f32[4,4,2,512,192]{3,4,1,2,0:T(8,128)} %bitcast.40) | data formatting | bytes 25165824 | tf_op jit(solution)/shard_map/transpose | solution.py:22
  29.9 0.0 reduce-scatter.7.cloned.1.call-update
  29.9 0.0 reduce-scatter.5.cloned.1.call-start
  30.0 230.7 %all-gather.3.cloned.1.call-done = bf16[512,6144]{0,1:T(8,128)(2,1)} async-done(((bf16[512,192]{0,1:T(8,128)(2,1)}), bf16[512,6144]{0,1:T(8,128)(2,1)}) %all-gather.3.cloned.1.call-update) | async-done | bytes 6291472 | tf_op jit(solution)/shard_map/all_gather | solution.py:65
  260.7 9.2 %fusion.14 = f32[6144,512]{1,0:T(8,128)} fusion(bf16[512,6144]{0,1:T(8,128)(2,1)} %all-gather.3.cloned.1.call-done, bf16[512,512]{1,0:T(8,128)(2,1)S(1)} %copy-done), kind=kOutput, calls=%fused_computation.29 | convolution fusion | flops 3221225472 | bytes 19398656 | tf_op jit(solution)/shard_map/dot_general | solution.py:64
  269.9 0.0 reduce-scatter.5.cloned.1.call-update
  269.9 0.0 reduce-scatter.9.cloned.1.call-start
  270.0 0.0 reduce-scatter.7.cloned.1.call-done
  270.0 0.5 reduce-scatter.9.cloned.1.call-update
  270.5 0.0 reduce-scatter.11.cloned.1.call-start
  270.6 103.8 %reduce-scatter.5.cloned.1.call-done = f32[1536,512]{1,0:T(8,128)} async-done(((f32[6144,512]{1,0:T(8,128)}), f32[1536,512]{1,0:T(8,128)}) %reduce-scatter.5.cloned.1.call-update) | async-done | bytes 3145744 | tf_op jit(solution)/shard_map/reduce_scatter | solution.py:76
  374.4 3.3 dynamic-slice_bitcast_fusion
  377.7 1.5 collective-permute-start
  379.2 59.1 %reduce-scatter.9.cloned.1.call-done = f32[2,512,192]{1,2,0:T(8,128)} async-done(((f32[8,512,192]{1,2,0:T(8,128)}), f32[2,512,192]{1,2,0:T(8,128)}) %reduce-scatter.9.cloned.1.call-update) | async-done | bytes 786448 | tf_op jit(solution)/shard_map/reduce_scatter | solution.py:24
  438.3 0.0 reduce-scatter.11.cloned.1.call-update
  438.3 0.2 all-gather.5.cloned.1.call-start
  438.6 0.7 collective-permute-done
  439.2 6.2 %multiply_reduce_fusion = (f32[]{:T(128)}, f32[1,768,1024]{2,1,0:T(8,128)}) fusion(f32[1,768,512]{2,1,0:T(8,128)S(1)} %get-tuple-element.7, f32[1,768,512]{2,1,0:T(8,128)} %bitcast.2, pred[]{:T(512)S(6)} %eq.6, f32[1,768,1024]{2,1,0:T(8,128)} %param.7), kind=kLoop, calls=%fused_computation.9 | loop fusion | flops 5505023 | bytes 9437189 | tf_op jit(solution)/shard_map/reduce_sum | solution.py:43
  446.2 4.3 fusion.6
  450.5 5.2 add_convert_fusion.1
  455.7 1.4 convolution_convert_fusion
  457.1 4.6 fusion.1
  461.6 2.9 reshape.82
  464.5 3.2 constant_dynamic-slice_fusion.1
  467.8 0.2 copy.21
  468.0 1.8 collective-permute-start.1
  469.8 0.2 copy.22
  470.0 17.0 %collective-permute-done.1 = bf16[768,512]{1,0:T(8,128)(2,1)S(1)} collective-permute-done((bf16[768,512]{1,0:T(8,128)(2,1)S(1)}, bf16[768,512]{1,0:T(8,128)(2,1)S(1)}, u32[]{:S(2)}, u32[]{:S(2)}) %collective-permute-start.1) | collective-permute-done | bytes 786464 | tf_op jit(solution)/shard_map/ppermute | solution.py:39
  486.9 1.8 maximum_select_fusion.1
  488.7 0.0 all-gather.5.cloned.1.call-update
  488.8 0.0 reduce-scatter.11.cloned.1.call-done
  488.8 1.7 convert_bitcast_fusion
  490.5 49.4 %all-gather.5.cloned.1.call-done = bf16[6144,512]{1,0:T(8,128)(2,1)} async-done(((bf16[1536,512]{1,0:T(8,128)(2,1)}), bf16[6144,512]{1,0:T(8,128)(2,1)}) %all-gather.5.cloned.1.call-update) | async-done | bytes 6291472 | tf_op jit(solution)/shard_map/all_gather | solution.py:97
  539.9 0.0 copy-start.1
  539.9 9.2 %subtract_convert_fusion = bf16[6144,512]{1,0:T(8,128)(2,1)} fusion(bf16[6144,512]{1,0:T(8,128)(2,1)} %all-gather.5.cloned.1.call-done, bf16[6144,512]{1,0:T(8,128)(2,1)} %param.6), kind=kLoop, calls=%fused_computation | loop fusion | flops 15728640 | bytes 18874368 | tf_op jit(solution)/shard_map/convert_element_type | solution.py:98
  549.1 0.0 copy-done.1
Async XLA Ops:
  8.0 1.1 copy-start
  8.0 252.7 %all-gather.3.cloned.1.call-start = ((), (), s32[]{:S(2)}) async-start(), calls=%async_computation.4 | async-start | bytes 6488064 | tf_op jit(solution)/shard_map/all_gather | solution.py:65
  8.7 261.3 %reduce-scatter.7.cloned.1.call-start = ((), (), s32[]{:S(2)}) async-start(), calls=%async_computation.7 | async-start | bytes 15728640 | tf_op jit(solution)/shard_map/reduce_scatter | solution.py:24
  29.9 344.5 %reduce-scatter.5.cloned.1.call-start = ((), (), s32[]{:S(2)}) async-start(), calls=%async_computation.5 | async-start | bytes 15728640 | tf_op jit(solution)/shard_map/reduce_scatter | solution.py:76
  269.9 168.4 %reduce-scatter.9.cloned.1.call-start = ((), (), s32[]{:S(2)}) async-start(), calls=%async_computation.8 | async-start | bytes 3932160 | tf_op jit(solution)/shard_map/reduce_scatter | solution.py:24
  270.5 218.3 %reduce-scatter.11.cloned.1.call-start = ((), (), s32[]{:S(2)}) async-start(), calls=%async_computation.9 | async-start | bytes 1179648 | tf_op jit(solution)/shard_map/reduce_scatter | solution.py:24
  377.7 61.5 %collective-permute-start = (f32[768,512]{1,0:T(8,128)}, f32[768,512]{1,0:T(8,128)}, u32[]{:S(2)}, u32[]{:S(2)}) collective-permute-start(f32[768,512]{1,0:T(8,128)} %get-tuple-element.6), channel_id=1, source_target_pairs={{0,1},{1,0},{2,3},{3,2},{4,5},{5,4},{6,7},{7,6},{8,9},{9,8},{10,11... | collective-permute-start | bytes 4718600 | tf_op jit(solution)/shard_map/ppermute | solution.py:39
  438.3 101.6 %all-gather.5.cloned.1.call-start = ((), (), s32[]{:S(2)}) async-start(), calls=%async_computation.6 | async-start | bytes 7864320 | tf_op jit(solution)/shard_map/all_gather | solution.py:97
  468.0 19.0 %collective-permute-start.1 = (bf16[768,512]{1,0:T(8,128)(2,1)S(1)}, bf16[768,512]{1,0:T(8,128)(2,1)S(1)}, u32[]{:S(2)}, u32[]{:S(2)}) collective-permute-start(bf16[768,512]{1,0:T(8,128)(2,1)S(1)} %bitcast.44), channel_id=1, source_target_pairs={{0,1},{1,0},{2,3},{3,2},{4,5},{5,4},{6,7},{7,6},{8,9},{9,8},{10,11... | collective-permute-start | bytes 2359304 | tf_op jit(solution)/shard_map/ppermute | solution.py:39
  539.9 9.2 %copy-start.1 = (bf16[512,512]{1,0:T(8,128)(2,1)S(1)}, bf16[512,512]{1,0:T(8,128)(2,1)}, u32[]{:S(2)}) copy-start(bf16[512,512]{1,0:T(8,128)(2,1)} %param.5) | copy-start | bytes 1572868
Sparse Core Ops, SparseCore 0:
  10.5 250.2 all-gather.2
Sparse Core Ops, SparseCore 1:
  30.0 128.2 reduce-scatter.6
  270.0 104.3 reduce-scatter.4
  376.7 61.6 reduce-scatter.8
  440.7 20.3 reduce-scatter.10
  488.8 51.0 all-gather.4
where the time goes:
time: 558 us; the launch traced here: 557 us
  waiting for transfers between devices  462 us (83%)
  matrix products  33.8 us (6%)
  local copies, waits for them, and re-layouts  21.7 us (4%)
  other arithmetic  18.9 us (3%)
  between operations  16.5 us (3%)
    all_gather x1, waiting for transfers between devices, body(): lax.all_gather(tokens, COLS, axis=1, tiled=True)  231 us
    reduce_scatter x1, waiting for transfers between devices, body(): lax.psum_scatter(partial_value, 'rows', scatter_dimension=0, tiled=True)  104 us
    reduce_scatter x3, waiting for transfers between devices, reduced_to_own(): pieces = lax.psum_scatter(pieces, axes[k], scatter_dimension=0, tiled=True)  59.2 us
    all_gather x1, waiting for transfers between devices, body(): placed = lax.all_gather(stacked, 'rows', axis=0, tiled=True)  49.4 us
    ppermute x2, waiting for transfers between devices, partner(): lax.ppermute(x, axis, [(i, i ^ 1 << bit) for i in range(lax.axis_size(axi...  17.6 us
    transpose x1, local copies, waits for them, and re-layouts, reduced_to_own(): jnp.moveaxis(pieces, sequence, range(len(axes))).reshape(-1, *inside)  11.6 us
  transfers between devices with their start and end apart: 8, of which 6 were waited for; matrix products, arithmetic and copies ran while one was open for 12% of the time, Pallas kernels for 0%

commit v1 on v0

v1 whole, which is shorter than its diff:
```python
import functools

import jax
import jax.numpy as jnp
from jax import lax
from jax.experimental import pallas as pl
from jax.experimental.pallas import tpu as pltpu
from jax.sharding import PartitionSpec as P

NS_STEPS = 2
TOK = 512
FEAT = 192
BR = 768
BC = 1024
HALF = 512
COEF_A = 3.4445
COEF_B = -4.775
COEF_C = 2.0315
BETA = 0.95

MESH = pl.DeviceIdType.MESH
F32 = jnp.float32
BF16 = jnp.bfloat16


def place():
    r = lax.axis_index("rows")
    c = lax.axis_index("cols")
    return r, c, c // 8, (c // 4) % 2, c % 4


def remote(src, dst, send, recv, r, c):
    return pltpu.make_async_remote_copy(
        src_ref=src,
        dst_ref=dst,
        send_sem=send,
        recv_sem=recv,
        device_id=(r, c),
        device_id_type=MESH,
    )


def spread_targets():
    r, c, x, zl, y = place()
    out = []
    for zd in range(2):
        for yb in range(2):
            col = r * 8 + zd * 4 + zl + 2 * yb
            out.append((x, col, (x == r) & (col == c)))
    return out


def spread_sources():
    r, c, x, zl, y = place()
    return [(x, r * 8 + (y % 2) * 4 + k, (x == r) & (r * 8 + (y % 2) * 4 + k == c)) for k in range(4)]


def x_neighbours():
    r, c, x, zl, y = place()
    low = c % 8
    return ((x + 3) % 4) * 8 + low, ((x + 1) % 4) * 8 + low


def signal_unless(flag, barrier, r, c):
    @pl.when(jnp.logical_not(flag))
    def _():
        pl.semaphore_signal(barrier, inc=1, device_id=(r, c), device_id_type=MESH)


def entry_barrier():
    r, c, x, zl, y = place()
    left, right = x_neighbours()
    barrier = pltpu.get_barrier_semaphore()
    for rd, cd in ((r, left), (r, right), (r ^ 2, c), (r, c ^ 1), (r ^ 2, c ^ 1), (r ^ 1, c)):
        pl.semaphore_signal(barrier, inc=1, device_id=(rd, cd), device_id_type=MESH)
    targets, sources = spread_targets(), spread_sources()
    for rd, cd, own in targets + sources:
        signal_unless(own, barrier, rd, cd)
    own_count = sum(jnp.where(own, 1, 0) for _, _, own in targets + sources)
    pl.semaphore_wait(barrier, 14 - own_count)


def gather_kernel(
    tok_ref, cot_ref, w_ref, grad_ref, terms_ref,
    tokg, cotg, wcat, gacc, tbuf,
    s1s, s1r, xs, xr, cs, cr, ds_, dr, ws, wr, ls, os_,
):
    r, c, x, zl, y = place()
    h = c % 2
    o = 1 - h
    left, right = x_neighbours()
    entry_barrier()

    def rows_of(group):
        return pl.ds(pl.multiple_of(group * TOK, TOK), TOK)

    def half_of(which):
        return pl.ds(pl.multiple_of(which * HALF, HALF), HALF)

    sends = []
    for k, (rd, cd, own) in enumerate(spread_targets()):
        dst = tokg.at[pl.ds(pl.multiple_of(y * FEAT, FEAT), FEAT), rows_of(r)]
        cp = remote(tok_ref, dst, s1s.at[k], s1r.at[y], rd, cd)
        here = pltpu.make_async_copy(tok_ref, dst, s1r.at[y])

        @pl.when(jnp.logical_not(own))
        def _():
            cp.start()

        @pl.when(own)
        def _():
            here.start()

        sends.append((cp, own))

    mine = cotg.at[rows_of(r), half_of(h)]
    peers = ((r, c ^ 1), (r ^ 2, c), (r ^ 2, c ^ 1))
    direct = []
    for k, (rd, cd) in enumerate(peers):
        cp = remote(cot_ref, mine, cs.at[k], cr.at[k], rd, cd)
        cp.start()
        direct.append(cp)
    core = [remote(cot_ref, mine, ds_.at[3], dr.at[3], r ^ 1, c)]
    core[0].start()
    own_cot = pltpu.make_async_copy(cot_ref, mine, ls.at[0])
    own_cot.start()

    wsend = remote(
        w_ref.at[pl.ds(pl.multiple_of((2 * r + o) * BR, BR), BR), :],
        wcat.at[:, half_of(h)], ws.at[0], wr.at[0], r, c ^ 1,
    )
    wsend.start()
    own_w = pltpu.make_async_copy(
        w_ref.at[pl.ds(pl.multiple_of((2 * r + h) * BR, BR), BR), :], wcat.at[:, half_of(h)], ls.at[1]
    )
    own_w.start()

    ring = []
    for k in range(4):
        piece = tokg.at[pl.ds(k * FEAT, FEAT), rows_of(x)]
        pltpu.make_async_copy(piece, piece, s1r.at[k]).wait()
        for d, cd in ((0, left), (1, right)):
            cp = remote(piece, piece, xs.at[d, k], xr.at[d, k], r, cd)
            cp.start()
            ring.append(cp)

    froms = ((r, o), (r ^ 2, h), (r ^ 2, o))
    for k, (rs, hs) in enumerate(froms):
        ref = cotg.at[rows_of(rs), half_of(hs)]
        pltpu.make_async_copy(ref, ref, cr.at[k]).wait()
        cp = remote(ref, ref, ds_.at[k], dr.at[k], r ^ 1, c)
        cp.start()
        core.append(cp)

    xl, xr_ = (x + 3) % 4, (x + 1) % 4
    for k in range(2):
        ref = tokg.at[pl.ds(k * FEAT, FEAT), rows_of(xl)]
        pltpu.make_async_copy(ref, ref, xr.at[1, k]).wait()
        cp = remote(ref, ref, xs.at[2, k], xr.at[2, k], r, right)
        cp.start()
        ring.append(cp)
        ref = tokg.at[pl.ds((k + 2) * FEAT, FEAT), rows_of(xr_)]
        pltpu.make_async_copy(ref, ref, xr.at[0, k + 2]).wait()
        cp = remote(ref, ref, xs.at[2, k + 2], xr.at[2, k + 2], r, left)
        cp.start()
        ring.append(cp)

    own_cot.wait()
    for k, (rs, hs) in enumerate(((r ^ 1, o), (r ^ 3, h), (r ^ 3, o), (r ^ 1, h))):
        ref = cotg.at[rows_of(rs), half_of(hs)]
        pltpu.make_async_copy(ref, ref, dr.at[k]).wait()

    def grad_step(group, first):
        def tile(i, carry):
            rows = pl.ds(pl.multiple_of(i * 256, 256), 256)
            part = jnp.dot(tokg[rows, rows_of(group)], cotg[rows_of(group), :], preferred_element_type=F32)
            gacc[rows, :] = part if first else gacc[rows, :] + part
            return carry

        lax.fori_loop(0, BR // 256, tile, 0)

    grad_step(x, True)
    for k in range(2):
        ref = tokg.at[pl.ds(k * FEAT, FEAT), rows_of(xr_)]
        pltpu.make_async_copy(ref, ref, xr.at[0, k]).wait()
        ref = tokg.at[pl.ds((k + 2) * FEAT, FEAT), rows_of(xl)]
        pltpu.make_async_copy(ref, ref, xr.at[1, k + 2]).wait()
    grad_step(xl, False)
    grad_step(xr_, False)

    own_w.wait()
    pltpu.make_async_copy(wcat.at[:, half_of(o)], wcat.at[:, half_of(o)], wr.at[0]).wait()

    def terms_step(group, carry):
        def tile(i, inner):
            rows = pl.ds(pl.multiple_of(i * 256, 256), 256)
            part = lax.dot_general(
                wcat[rows, :], cotg[rows_of(group), :], (((1,), (1,)), ((), ())), preferred_element_type=F32
            )
            tbuf[rows, rows_of(group)] = part.astype(BF16)
            return inner

        return lax.fori_loop(0, BR // 256, tile, carry)

    lax.fori_loop(0, 4, terms_step, 0)
    out_terms = pltpu.make_async_copy(tbuf, terms_ref, os_.at[0])
    out_terms.start()

    x2 = (x + 2) % 4
    for k in range(4):
        ref = tokg.at[pl.ds(k * FEAT, FEAT), rows_of(x2)]
        pltpu.make_async_copy(ref, ref, xr.at[2, k]).wait()
    grad_step(x2, False)
    out_grad = pltpu.make_async_copy(gacc, grad_ref, os_.at[1])
    out_grad.start()

    for cp, own in sends:
        @pl.when(jnp.logical_not(own))
        def _():
            cp.wait_send()
    for cp in ring + direct + core + [wsend]:
        cp.wait_send()
    out_terms.wait()
    out_grad.wait()


def gather_call(tok, cot, weight):
    any_ = pl.BlockSpec(memory_space=pl.ANY)
    dma = pltpu.SemaphoreType.DMA
    return pl.pallas_call(
        gather_kernel,
        out_shape=(
            jax.ShapeDtypeStruct((BR, BC), F32),
            jax.ShapeDtypeStruct((BR, 4 * TOK), BF16),
        ),
        in_specs=[any_, any_, any_],
        out_specs=(any_, any_),
        scratch_shapes=[
            pltpu.VMEM((BR, 4 * TOK), BF16),
            pltpu.VMEM((4 * TOK, BC), BF16),
            pltpu.VMEM((BR, BC), BF16),
            pltpu.VMEM((BR, BC), F32),
            pltpu.VMEM((BR, 4 * TOK), BF16),
            dma((4,)), dma((4,)), dma((3, 4)), dma((3, 4)), dma((3,)), dma((3,)),
            dma((4,)), dma((4,)), dma((1,)), dma((1,)), dma((2,)), dma((2,)),
        ],
        compiler_params=pltpu.CompilerParams(
            collective_id=0, has_side_effects=True, vmem_limit_bytes=48 << 20
        ),
        cost_estimate=pl.CostEstimate(flops=7_000_000_000, bytes_accessed=20_000_000, transcendentals=0),
        name="gather_dots",
    )(tok, cot, weight)


def tiles(step, rows=256):
    def run(i, carry):
        step(pl.ds(pl.multiple_of(i * rows, rows), rows))
        return carry

    lax.fori_loop(0, BR // rows, run, 0)


def ortho_kernel(grad_ref, mom_ref, newm_ref, upd_ref, x_ref, sq, ab, xb):
    sq[...] = jnp.zeros_like(sq)

    def momentum(rows):
        new = BETA * mom_ref[rows, :] + grad_ref[rows, :]
        newm_ref[rows, :] = new
        sq[...] += jnp.sum((new * new).reshape(-1, 8, BC), axis=0)

    tiles(momentum, 64)
    norm = jnp.sqrt(jnp.sum(sq[...])) + 1e-07

    def first(rows):
        x_ref[rows, :] = (newm_ref[rows, :] / norm).astype(BF16)

    tiles(first, 64)
    nt = (((1,), (1,)), ((), ()))
    src, dst = x_ref, xb
    for step in range(NS_STEPS):
        def gram(rows):
            ab[0, rows, :] = lax.dot_general(src[rows, :], src[...], nt, preferred_element_type=F32).astype(BF16)

        def poly(rows):
            a = ab[0, rows, :]
            aa = jnp.dot(a, ab[0], preferred_element_type=F32)
            ab[1, rows, :] = (COEF_B * a.astype(F32) + COEF_C * aa).astype(BF16)

        last = step == NS_STEPS - 1

        def apply(rows):
            bx = jnp.dot(ab[1, rows, :], src[...], preferred_element_type=F32)
            new = (COEF_A * src[rows, :].astype(F32) + bx).astype(BF16)
            dst[rows, :] = new
            if last:
                upd_ref[rows, :] = 32.0 * new.astype(F32)

        tiles(gram)
        tiles(poly)
        tiles(apply)
        src, dst = dst, src


def ortho_call(grad, momentum):
    vm = pl.BlockSpec(memory_space=pltpu.VMEM)
    return pl.pallas_call(
        ortho_kernel,
        out_shape=(
            jax.ShapeDtypeStruct((BR, BC), F32),
            jax.ShapeDtypeStruct((BR, BC), F32),
            jax.ShapeDtypeStruct((BR, BC), BF16),
        ),
        in_specs=[vm, vm],
        out_specs=(vm, vm, vm),
        scratch_shapes=[
            pltpu.VMEM((8, BC), F32),
            pltpu.VMEM((2, BR, BR), BF16),
            pltpu.VMEM((BR, BC), BF16),
        ],
        compiler_params=pltpu.CompilerParams(vmem_limit_bytes=40 << 20),
        cost_estimate=pl.CostEstimate(flops=7_000_000_000, bytes_accessed=14_000_000, transcendentals=0),
        name="momentum_ortho",
    )(grad, momentum)


def scatter_kernel(
    terms_ref, x_ref, w_ref, ig_ref, neww_ref,
    tb, fl, fr, sb, ib, igb, ub, wb,
    xs, xr, cs, cr, ds_, dr, s2s, s2r, ls, os_,
):
    r, c, x, zl, y = place()
    h = c % 2
    o = 1 - h
    left, right = x_neighbours()
    load_w = pltpu.make_async_copy(w_ref, wb, ls.at[0])
    load_w.start()
    load_t = pltpu.make_async_copy(terms_ref, tb, ls.at[1])
    load_t.start()
    entry_barrier()

    def rows_of(group):
        return pl.ds(pl.multiple_of(group * TOK, TOK), TOK)

    def half_of(which):
        return pl.ds(pl.multiple_of(which * HALF, HALF), HALF)

    xl, xr_, x2 = (x + 3) % 4, (x + 1) % 4, (x + 2) % 4
    MID = BR // 2
    top, low = pl.ds(0, MID), pl.ds(MID, MID)

    own_x = x_ref.at[:, half_of(h)]
    other_x = x_ref.at[:, half_of(o)]
    slot = ub.at[2 * r + h]
    direct = []
    for k, (src, rd, cd) in enumerate(((other_x, r, c ^ 1), (own_x, r ^ 2, c), (other_x, r ^ 2, c ^ 1))):
        cp = remote(src, slot, cs.at[k], cr.at[k], rd, cd)
        cp.start()
        direct.append(cp)
    core = [remote(own_x, slot, ds_.at[3], dr.at[3], r ^ 1, c)]
    core[0].start()
    own_u = pltpu.make_async_copy(own_x, slot, ls.at[2])
    own_u.start()

    ring = []

    def send(src, dst, i, j, cd):
        cp = remote(src, dst, xs.at[i, j], xr.at[i, j], r, cd)
        cp.start()
        ring.append(cp)

    load_t.wait()
    send(tb.at[top, rows_of(x2)], fl.at[0], 0, 0, right)
    send(tb.at[low, rows_of(x2)], fr.at[0], 1, 0, left)
    send(tb.at[low, rows_of(xr_)], fl.at[2], 0, 1, right)
    send(tb.at[top, rows_of(xl)], fr.at[2], 1, 1, left)
    pltpu.make_async_copy(fl.at[0], fl.at[0], xr.at[0, 0]).wait()

    def join(src, rows, group):
        def step(i, carry):
            part = pl.ds(pl.multiple_of(i * 64, 64), 64)
            here = pl.ds(pl.multiple_of(rows + i * 64, 64), 64)
            src[0, part, :] = (
                src[0, part, :].astype(F32) + tb[here, rows_of(group)].astype(F32)
            ).astype(BF16)
            return carry

        lax.fori_loop(0, MID // 64, step, 0)

    join(fl, 0, xr_)
    send(fl.at[0], fl.at[1], 0, 2, right)
    pltpu.make_async_copy(fr.at[0], fr.at[0], xr.at[1, 0]).wait()
    join(fr, MID, xl)
    send(fr.at[0], fr.at[1], 1, 2, left)

    def update_rows(rs, hs):
        at = 2 * rs + hs

        def step(i, carry):
            part = pl.ds(pl.multiple_of(i * 64, 64), 64)
            here = pl.ds(pl.multiple_of(at * BR + i * 64, 64), 64)
            wb[here, :] = (wb[here, :].astype(F32) - 8.0 * ub[at, part, :].astype(F32)).astype(BF16)
            return carry

        lax.fori_loop(0, BR // 64, step, 0)
        rows = pl.ds(pl.multiple_of(at * BR, BR), BR)
        cp = pltpu.make_async_copy(wb.at[rows, :], neww_ref.at[rows, :], os_.at[at])
        cp.start()
        return cp

    outs = []
    load_w.wait()
    own_u.wait()
    outs.append(update_rows(r, h))
    pltpu.make_async_copy(slot, slot, dr.at[3]).wait()
    outs.append(update_rows(r ^ 1, h))

    for ref, i, j in ((fl, 0, 1), (fr, 1, 1), (fl, 0, 2), (fr, 1, 2)):
        at = 2 if j == 1 else 1
        pltpu.make_async_copy(ref.at[at], ref.at[at], xr.at[i, j]).wait()

    def total(i, carry):
        part = pl.ds(pl.multiple_of(i * 64, 64), 64)
        below = pl.ds(pl.multiple_of(MID + i * 64, 64), 64)
        sb[part, :] = (
            tb[part, rows_of(x)].astype(F32) + fl[1, part, :].astype(F32) + fr[2, part, :].astype(F32)
        ).astype(BF16)
        sb[below, :] = (
            tb[below, rows_of(x)].astype(F32) + fr[1, part, :].astype(F32) + fl[2, part, :].astype(F32)
        ).astype(BF16)
        return carry

    lax.fori_loop(0, MID // 64, total, 0)
    last = []
    for k, (rd, cd, own) in enumerate(spread_sources()):
        piece = sb.at[pl.ds(k * FEAT, FEAT), :]
        at = zl * 2 + y // 2
        cp = remote(piece, ib.at[at], s2s.at[k], s2r.at[at], rd, cd)
        here = pltpu.make_async_copy(piece, ib.at[at], s2r.at[at])

        @pl.when(jnp.logical_not(own))
        def _():
            cp.start()

        @pl.when(own)
        def _():
            here.start()

        last.append((cp, own))

    froms = ((r, o), (r ^ 2, h), (r ^ 2, o))
    for k, (rs, hs) in enumerate(froms):
        ref = ub.at[2 * rs + hs]
        pltpu.make_async_copy(ref, ref, cr.at[k]).wait()
        cp = remote(ref, ref, ds_.at[k], dr.at[k], r ^ 1, c)
        cp.start()
        core.append(cp)
        outs.append(update_rows(rs, hs))

    for k in range(4):
        pltpu.make_async_copy(ib.at[k], ib.at[k], s2r.at[k]).wait()
    igb[...] = (
        (ib[0].astype(F32) + ib[1].astype(F32)) + (ib[2].astype(F32) + ib[3].astype(F32))
    ).astype(BF16)
    out_ig = pltpu.make_async_copy(igb, ig_ref, os_.at[8])
    out_ig.start()

    for k, (rs, hs) in enumerate(((r ^ 1, o), (r ^ 3, h), (r ^ 3, o))):
        ref = ub.at[2 * rs + hs]
        pltpu.make_async_copy(ref, ref, dr.at[k]).wait()
        outs.append(update_rows(rs, hs))

    for cp, own in last:
        @pl.when(jnp.logical_not(own))
        def _():
            cp.wait_send()
    for cp in ring + direct + core:
        cp.wait_send()
    for cp in outs:
        cp.wait()
    out_ig.wait()


def scatter_call(terms, xmat, weight):
    any_ = pl.BlockSpec(memory_space=pl.ANY)
    dma = pltpu.SemaphoreType.DMA
    return pl.pallas_call(
        scatter_kernel,
        out_shape=(
            jax.ShapeDtypeStruct((FEAT, TOK), BF16),
            jax.ShapeDtypeStruct(weight.shape, BF16),
        ),
        in_specs=[any_, pl.BlockSpec(memory_space=pltpu.VMEM), any_],
        out_specs=(any_, any_),
        scratch_shapes=[
            pltpu.VMEM((BR, 4 * TOK), BF16),
            pltpu.VMEM((3, BR // 2, TOK), BF16),
            pltpu.VMEM((3, BR // 2, TOK), BF16),
            pltpu.VMEM((BR, TOK), BF16),
            pltpu.VMEM((4, FEAT, TOK), BF16),
            pltpu.VMEM((FEAT, TOK), BF16),
            pltpu.VMEM((8, BR, HALF), BF16),
            pltpu.VMEM(weight.shape, BF16),
            dma((2, 3)), dma((2, 3)), dma((3,)), dma((3,)), dma((4,)), dma((4,)),
            dma((4,)), dma((4,)), dma((3,)), dma((9,)),
        ],
        compiler_params=pltpu.CompilerParams(
            collective_id=1, has_side_effects=True, vmem_limit_bytes=48 << 20
        ),
        cost_estimate=pl.CostEstimate(flops=20_000_000, bytes_accessed=20_000_000, transcendentals=0),
        name="scatter_update",
    )(terms, xmat, weight)


def body(tokens, cotangent, weight, momentum):
    grad, terms = gather_call(tokens.T, cotangent, weight)
    new_momentum, update, xmat = ortho_call(grad, momentum[0])
    input_grad, new_weight = scatter_call(terms, xmat, weight)
    return new_weight, input_grad.T, new_momentum[None], update[None]


def solution(mesh):
    in_specs = (P("rows", "cols"), P("rows", "cols"), P(None, "cols"), P(("rows", "cols"), None, None))
    out_specs = (
        P(None, "cols"),
        P("rows", "cols"),
        P(("rows", "cols"), None, None),
        P(("rows", "cols"), None, None),
    )
    return jax.shard_map(body, mesh=mesh, in_specs=in_specs, out_specs=out_specs, check_vma=False)
```

time: 558 us -> 176 us (0.32)
  waiting for transfers between devices: 462 us -> 0 us
  Pallas kernels: 0 us -> 164 us
  matrix products: 33.8 us -> 0 us
  other arithmetic: 18.9 us -> 0 us
  between operations: 16.5 us -> 0.67 us
  local copies, waits for them, and re-layouts: 21.7 us -> 8.54 us
    all_gather x2 -> x0, waiting for transfers between devices: 280 us -> none  [the longest x1 231 us: body(): lax.all_gather(tokens, COLS, axis=1, tiled=True)]
    pallas_call x0 -> x3, Pallas kernels: none -> 164 us  [the longest x1 81.4 us: gather_call(): pl.pallas_call(gather_kernel, out_shape=(jax.ShapeDtypeStruct((BR, BC), F...]
    reduce_scatter x4 -> x0, waiting for transfers between devices: 163 us -> none  [the longest x1 104 us: body(): lax.psum_scatter(partial_value, 'rows', scatter_dimension=0, tiled=True)]
    dot_general x6 -> x0, matrix products: 33.8 us -> none  [the longest x2 9.74 us: orthogonalize(): jnp.dot(poly, current, preferred_element_type=jnp.float32)]
    ppermute x2 -> x0, waiting for transfers between devices: 17.6 us -> none  [partner(): lax.ppermute(x, axis, [(i, i ^ 1 << bit) for i in range(lax.axis_size(axi...]
    transpose x1 -> x0, local copies, waits for them, and re-layouts: 11.6 us -> none  [reduced_to_own(): jnp.moveaxis(pieces, sequence, range(len(axes))).reshape(-1, *inside)]
    convert_element_type x2 -> x0, other arithmetic: 10.9 us -> none  [the longest x1 9.18 us: body(): (weight.astype(jnp.float32) - step_rate * placed.astype(jnp.float32)).ast...]
    unnamed x6 -> x10, local copies, waits for them, and re-layouts: 0.67 us -> 8.54 us
  transfers between devices with their start and end apart: 8 -> 0, of which waited for: 6 -> 0; matrix products, arithmetic and copies ran while one was open for 12% -> 0% of each run, Pallas kernels for 0% -> 0%
where the time goes in v1:
time: 176 us; the launch traced here: 173 us
  Pallas kernels  164 us (93%)
  local copies, waits for them, and re-layouts  8.54 us (5%)
    pallas_call x1, Pallas kernels, gather_call(): pl.pallas_call(gather_kernel, out_shape=(jax.ShapeDtypeStruct((BR, BC), F...  81.4 us
    pallas_call x1, Pallas kernels, scatter_call(): pl.pallas_call(scatter_kernel, out_shape=(jax.ShapeDtypeStruct((FEAT, TOK...  69.1 us
    pallas_call x1, Pallas kernels, ortho_call(): pl.pallas_call(ortho_kernel, out_shape=(jax.ShapeDtypeStruct((BR, BC), F3...  13.2 us
    unnamed x10, local copies, waits for them, and re-layouts  8.54 us

profile of v1, /device:TPU:0, one launch (start us, length us, event | category | flops | bytes accessed | tf_op | source)
XLA Modules:
  0.0 172.9 jit_solution(7817491822570305729)
XLA Ops:
  0.6 0.0 copy-start.2
  0.6 1.0 copy-done.2
  1.7 0.0 copy-start.3
  1.7 0.9 copy-done.3
  2.6 0.0 copy-start.1
  2.6 81.4 %gather_dots.1 = (f32[768,1024]{1,0:T(8,128)S(1)}, bf16[768,2048]{1,0:T(8,128)(2,1)}) custom-call(bf16[192,512]{1,0:T(8,128)(2,1)S(1)} %bitcast.7, bf16[512,512]{1,0:T(8,128)(2,1)S(1)} %copy-done.2, bf16[6144,512]{1,0:T(8,128)(2,1)} %w_ref.3), custom_call_target="tpu_custom_call" | custom-call | flops 7000000000 | bytes 20000000 | tf_op jit(solution)/shard_map/gather_dots/pallas_call | solution.py:230
  84.0 0.0 copy-done.1
  84.0 0.0 copy-start
  84.0 13.2 %momentum_ortho.1 = (f32[768,1024]{1,0:T(8,128)}, f32[768,1024]{1,0:T(8,128)}, bf16[768,1024]{1,0:T(8,128)(2,1)S(1)}) custom-call(f32[768,1024]{1,0:T(8,128)S(1)} %get-tuple-element.12.grad_ref, f32[768,1024]{1,0:T(8,128)S(1)} %bitcast.6), custom_call_target="tpu_custom_call" | custom-call | flops 7000000000 | bytes 14000000 | tf_op jit(solution)/shard_map/momentum_ortho/pallas_call | solution.py:306
  97.2 0.0 copy-done
  97.3 69.1 %scatter_update.1 = (bf16[192,512]{1,0:T(8,128)(2,1)S(1)}, bf16[6144,512]{1,0:T(8,128)(2,1)}) custom-call(bf16[768,2048]{1,0:T(8,128)(2,1)S(1)} %copy-done, bf16[768,1024]{1,0:T(8,128)(2,1)S(1)} %get-tuple-element.13.x_ref, bf16[6144,512]{1,0:T(8,128)(2,1)} %w_ref.3), custom_call_target="tpu_custom_call" | custom-call | flops 20000000 | bytes 20000000 | tf_op jit(solution)/shard_map/scatter_update/pallas_call | solution.py:486
  166.3 5.9 %copy.10 = bf16[6144,512]{1,0:T(8,128)(2,1)} copy(bf16[6144,512]{1,0:T(8,128)(2,1)} %get-tuple-element.22) | data formatting | bytes 12582912
  172.2 0.7 copy.11
Async XLA Ops:
  0.6 1.0 copy-start.2
  1.7 0.9 copy-start.3
  2.6 81.4 %copy-start.1 = (f32[1,768,1024]{2,1,0:T(8,128)S(1)}, f32[1,768,1024]{2,1,0:T(8,128)}, u32[]{:S(2)}) copy-start(f32[1,768,1024]{2,1,0:T(8,128)} %param.7) | copy-start | bytes 9437188
  84.0 13.2 %copy-start = (bf16[768,2048]{1,0:T(8,128)(2,1)S(1)}, bf16[768,2048]{1,0:T(8,128)(2,1)}, u32[]{:S(2)}) copy-start(bf16[768,2048]{1,0:T(8,128)(2,1)} %get-tuple-element.11.terms_ref) | copy-start | bytes 9437188

commit v2 on v1

v2 whole, which is shorter than its diff:
```python
import functools

import jax
import jax.numpy as jnp
from jax import lax
from jax.experimental import pallas as pl
from jax.experimental.pallas import tpu as pltpu
from jax.sharding import PartitionSpec as P

NS_STEPS = 2
TOK = 512
FEAT = 192
BR = 768
BC = 1024
HALF = 512
COEF_A = 3.4445
COEF_B = -4.775
COEF_C = 2.0315
BETA = 0.95

MESH = pl.DeviceIdType.MESH
F32 = jnp.float32
BF16 = jnp.bfloat16


def place():
    r = lax.axis_index("rows")
    c = lax.axis_index("cols")
    return r, c, c // 8, (c // 4) % 2, c % 4


def remote(src, dst, send, recv, r, c):
    return pltpu.make_async_remote_copy(
        src_ref=src,
        dst_ref=dst,
        send_sem=send,
        recv_sem=recv,
        device_id=(r, c),
        device_id_type=MESH,
    )


def flip(v):
    return (v % 2) * 2 + v // 2


def group_at(x, r):
    return flip((x + 4 - r) % 4)


def spread_targets():
    r, c, x, zl, y = place()
    out = []
    for zd in range(2):
        for yb in range(2):
            col = ((x + flip(r)) % 4) * 8 + zd * 4 + zl + 2 * yb
            out.append((x, col, (x == r) & (col == c)))
    return out


def spread_sources():
    r, c, x, zl, y = place()
    group = group_at(x, r)
    base = r * 8 + (y % 2) * 4
    return [(group, base + k, (group == r) & (base + k == c)) for k in range(4)]


def x_neighbours():
    r, c, x, zl, y = place()
    low = c % 8
    return ((x + 3) % 4) * 8 + low, ((x + 1) % 4) * 8 + low


def signal_unless(flag, barrier, r, c):
    @pl.when(jnp.logical_not(flag))
    def _():
        pl.semaphore_signal(barrier, inc=1, device_id=(r, c), device_id_type=MESH)


def entry_barrier():
    r, c, x, zl, y = place()
    left, right = x_neighbours()
    barrier = pltpu.get_barrier_semaphore()
    for rd, cd in ((r, left), (r, right), (r ^ 2, c), (r, c ^ 1), (r ^ 1, c)):
        pl.semaphore_signal(barrier, inc=1, device_id=(rd, cd), device_id_type=MESH)
    targets, sources = spread_targets(), spread_sources()
    for rd, cd, own in targets + sources:
        signal_unless(own, barrier, rd, cd)
    own_count = sum(jnp.where(own, 1, 0) for _, _, own in targets + sources)
    pl.semaphore_wait(barrier, 13 - own_count)


def rows_of(group):
    return pl.ds(pl.multiple_of(group * TOK, TOK), TOK)


def half_of(which):
    return pl.ds(pl.multiple_of(which * HALF, HALF), HALF)


def arrived(ref, sem):
    pltpu.make_async_copy(ref, ref, sem).wait()


def tiles(step, rows=256):
    def run(i, carry):
        step(pl.ds(pl.multiple_of(i * rows, rows), rows))
        return carry

    lax.fori_loop(0, BR // rows, run, 0)


def gather_kernel(
    tok_ref, cot_ref, w_ref, grad_ref, terms_ref,
    tokv, tokg, cotg, wcat, gacc, tacc,
    s1s, s1r, xs, xr, cs, cr, ds_, dr, ws, wr, ls,
):
    r, c, x, zl, y = place()
    h = c % 2
    o = 1 - h
    left, right = x_neighbours()
    mine = cotg.at[rows_of(r), half_of(h)]
    own_tok = pltpu.make_async_copy(tok_ref, tokv, ls.at[0])
    own_cot = pltpu.make_async_copy(cot_ref, mine, ls.at[1])
    own_w = pltpu.make_async_copy(
        w_ref.at[pl.ds(pl.multiple_of((2 * r + h) * BR, BR), BR), :], wcat.at[:, half_of(h)], ls.at[2]
    )
    own_tok.start()
    own_cot.start()
    own_w.start()
    entry_barrier()
    own_tok.wait()

    sends = []
    for k, (rd, cd, own) in enumerate(spread_targets()):
        dst = tokg.at[pl.ds(pl.multiple_of(y * FEAT, FEAT), FEAT), rows_of(r)]
        cp = remote(tokv, dst, s1s.at[k], s1r.at[y], rd, cd)
        here = pltpu.make_async_copy(tokv, dst, s1r.at[y])

        @pl.when(jnp.logical_not(own))
        def _():
            cp.start()

        @pl.when(own)
        def _():
            here.start()

        sends.append((cp, own))

    own_cot.wait()
    others = []

    def send(src, dst, ss, rs, rd, cd):
        cp = remote(src, dst, ss, rs, rd, cd)
        cp.start()
        others.append(cp)

    send(mine, mine, cs.at[0], cr.at[0], r, c ^ 1)
    send(mine, mine, cs.at[1], cr.at[1], r ^ 2, c)
    send(mine, mine, ds_.at[3], dr.at[3], r ^ 1, c)

    send(
        w_ref.at[pl.ds(pl.multiple_of((2 * r + o) * BR, BR), BR), :],
        wcat.at[:, half_of(h)], ws.at[0], wr.at[0], r, c ^ 1,
    )

    q0, ql, qr, q2 = (group_at((x + k) % 4, r) for k in (0, 3, 1, 2))
    for k in range(4):
        piece = tokg.at[pl.ds(k * FEAT, FEAT), rows_of(q0)]
        arrived(piece, s1r.at[k])
        send(piece, piece, xs.at[0, k], xr.at[0, k], r, left)
        send(piece, piece, xs.at[1, k], xr.at[1, k], r, right)

    froms = ((r, o), (r ^ 2, h), (r ^ 2, o))

    def pass_on(k):
        ref = cotg.at[rows_of(froms[k][0]), half_of(froms[k][1])]
        arrived(ref, cr.at[k])
        if k == 0:
            send(ref, ref, cs.at[2], cr.at[2], r ^ 2, c)
        send(ref, ref, ds_.at[k], dr.at[k], r ^ 1, c)

    pass_on(0)
    pass_on(1)

    for k in range(2):
        ref = tokg.at[pl.ds(k * FEAT, FEAT), rows_of(ql)]
        arrived(ref, xr.at[1, k])
        send(ref, ref, xs.at[2, k], xr.at[2, k], r, right)
        ref = tokg.at[pl.ds((k + 2) * FEAT, FEAT), rows_of(qr)]
        arrived(ref, xr.at[0, k + 2])
        send(ref, ref, xs.at[2, k + 2], xr.at[2, k + 2], r, left)

    def from_core(k, rs, hs):
        arrived(cotg.at[rows_of(rs), half_of(hs)], dr.at[k])

    own_w.wait()
    from_core(3, r ^ 1, h)
    from_core(1, r ^ 3, h)
    nt = (((1,), (1,)), ((), ()))

    def terms_half(which, first):
        def step(group, carry):
            def tile(rows):
                part = lax.dot_general(
                    wcat[rows, half_of(which)], cotg[rows_of(group), half_of(which)], nt,
                    preferred_element_type=F32,
                )
                if first:
                    tacc[rows, rows_of(group)] = part
                else:
                    terms_ref[rows, rows_of(group)] = (tacc[rows, rows_of(group)] + part).astype(BF16)

            tiles(tile)
            return carry

        lax.fori_loop(0, 4, step, 0)

    terms_half(h, True)
    pass_on(2)
    from_core(0, r ^ 1, o)
    from_core(2, r ^ 3, o)

    def grad_step(group, first, last=False):
        def tile(rows):
            part = jnp.dot(tokg[rows, rows_of(group)], cotg[rows_of(group), :], preferred_element_type=F32)
            total = part if first else gacc[rows, :] + part
            if last:
                grad_ref[rows, :] = total
            else:
                gacc[rows, :] = total

        tiles(tile)

    grad_step(q0, True)
    for k in range(2):
        arrived(tokg.at[pl.ds(k * FEAT, FEAT), rows_of(qr)], xr.at[0, k])
        arrived(tokg.at[pl.ds((k + 2) * FEAT, FEAT), rows_of(ql)], xr.at[1, k + 2])
    grad_step(ql, False)
    grad_step(qr, False)
    arrived(wcat.at[:, half_of(o)], wr.at[0])
    terms_half(o, False)
    for k in range(4):
        arrived(tokg.at[pl.ds(k * FEAT, FEAT), rows_of(q2)], xr.at[2, k])
    grad_step(q2, False, True)

    for cp, own in sends:
        @pl.when(jnp.logical_not(own))
        def _():
            cp.wait_send()
    for cp in others:
        cp.wait_send()


def gather_call(tok, cot, weight):
    hbm = pl.BlockSpec(memory_space=pltpu.HBM)
    vm = pl.BlockSpec(memory_space=pltpu.VMEM)
    dma = pltpu.SemaphoreType.DMA
    return pl.pallas_call(
        gather_kernel,
        out_shape=(
            jax.ShapeDtypeStruct((BR, BC), F32),
            jax.ShapeDtypeStruct((BR, 4 * TOK), BF16),
        ),
        in_specs=[hbm, hbm, hbm],
        out_specs=(vm, vm),
        scratch_shapes=[
            pltpu.VMEM((FEAT, TOK), BF16),
            pltpu.VMEM((BR, 4 * TOK), BF16),
            pltpu.VMEM((4 * TOK, BC), BF16),
            pltpu.VMEM((BR, BC), BF16),
            pltpu.VMEM((BR, BC), F32),
            pltpu.VMEM((BR, 4 * TOK), F32),
            dma((4,)), dma((4,)), dma((3, 4)), dma((3, 4)), dma((3,)), dma((3,)),
            dma((4,)), dma((4,)), dma((1,)), dma((1,)), dma((3,)),
        ],
        compiler_params=pltpu.CompilerParams(
            collective_id=0, has_side_effects=True, vmem_limit_bytes=48_000_000
        ),
        cost_estimate=pl.CostEstimate(flops=7_000_000_000, bytes_accessed=20_000_000, transcendentals=0),
        name="gather_dots",
    )(tok, cot, weight)


def ortho_scatter_kernel(
    grad_ref, mom_ref, terms_ref, w_ref, newm_ref, x_ref, ig_ref, neww_ref,
    sq, ab, xb, fl, fr, sb, ib, ub,
    xs, xr, cs, cr, ds_, dr, s2s, s2r, ls,
):
    r, c, x, zl, y = place()
    h = c % 2
    o = 1 - h
    left, right = x_neighbours()
    load_w = pltpu.make_async_copy(w_ref, neww_ref, ls.at[0])
    load_w.start()
    entry_barrier()
    q0, ql, qr, q2 = (group_at((x + k) % 4, r) for k in (0, 3, 1, 2))
    MID = BR // 2
    top, low = pl.ds(0, MID), pl.ds(MID, MID)
    others = []

    def send(src, dst, ss, rs, rd, cd):
        cp = remote(src, dst, ss, rs, rd, cd)
        cp.start()
        others.append(cp)

    send(terms_ref.at[top, rows_of(q2)], fl.at[0], xs.at[0, 0], xr.at[0, 0], r, right)
    send(terms_ref.at[low, rows_of(q2)], fr.at[0], xs.at[1, 0], xr.at[1, 0], r, left)
    send(terms_ref.at[low, rows_of(qr)], fl.at[2], xs.at[0, 1], xr.at[0, 1], r, right)
    send(terms_ref.at[top, rows_of(ql)], fr.at[2], xs.at[1, 1], xr.at[1, 1], r, left)

    def join(src, base, group):
        def step(i, carry):
            part = pl.ds(pl.multiple_of(i * 64, 64), 64)
            here = pl.ds(pl.multiple_of(base + i * 64, 64), 64)
            src[0, part, :] = (
                src[0, part, :].astype(F32) + terms_ref[here, rows_of(group)].astype(F32)
            ).astype(BF16)
            return carry

        lax.fori_loop(0, MID // 64, step, 0)

    sq[...] = jnp.zeros_like(sq)

    def momentum(rows):
        new = BETA * mom_ref[rows, :] + grad_ref[rows, :]
        newm_ref[rows, :] = new
        sq[...] += jnp.sum((new * new).reshape(-1, 8, BC), axis=0)

    tiles(momentum, 64)
    norm = jnp.sqrt(jnp.sum(sq[...])) + 1e-07

    def first(rows):
        x_ref[rows, :] = (newm_ref[rows, :] / norm).astype(BF16)

    tiles(first, 64)
    nt = (((1,), (1,)), ((), ()))
    src, dst = x_ref, xb
    for step in range(NS_STEPS):
        def gram(rows):
            ab[0, rows, :] = lax.dot_general(src[rows, :], src[...], nt, preferred_element_type=F32).astype(BF16)

        def poly(rows):
            a = ab[0, rows, :]
            aa = jnp.dot(a, ab[0], preferred_element_type=F32)
            ab[1, rows, :] = (COEF_B * a.astype(F32) + COEF_C * aa).astype(BF16)

        def apply(rows):
            bx = jnp.dot(ab[1, rows, :], src[...], preferred_element_type=F32)
            dst[rows, :] = (COEF_A * src[rows, :].astype(F32) + bx).astype(BF16)

        tiles(gram)
        tiles(poly)
        tiles(apply)
        if step == 0:
            arrived(fl.at[0], xr.at[0, 0])
            join(fl, 0, qr)
            send(fl.at[0], fl.at[1], xs.at[0, 2], xr.at[0, 2], r, right)
            arrived(fr.at[0], xr.at[1, 0])
            join(fr, MID, ql)
            send(fr.at[0], fr.at[1], xs.at[1, 2], xr.at[1, 2], r, left)
        src, dst = dst, src

    own_x = x_ref.at[:, half_of(h)]
    other_x = x_ref.at[:, half_of(o)]
    slot = ub.at[2 * r + h]
    send(other_x, slot, cs.at[0], cr.at[0], r, c ^ 1)
    send(own_x, slot, cs.at[1], cr.at[1], r ^ 2, c)
    send(own_x, slot, ds_.at[3], dr.at[3], r ^ 1, c)
    own_u = pltpu.make_async_copy(own_x, slot, ls.at[1])
    own_u.start()

    def update_rows(rs, hs):
        at = 2 * rs + hs

        def step(i, carry):
            part = pl.ds(pl.multiple_of(i * 64, 64), 64)
            here = pl.ds(pl.multiple_of(at * BR + i * 64, 64), 64)
            neww_ref[here, :] = (neww_ref[here, :].astype(F32) - 8.0 * ub[at, part, :].astype(F32)).astype(BF16)
            return carry

        lax.fori_loop(0, BR // 64, step, 0)

    load_w.wait()
    own_u.wait()
    update_rows(r, h)
    arrived(slot, dr.at[3])
    update_rows(r ^ 1, h)

    for ref, i, j in ((fl, 0, 1), (fr, 1, 1), (fl, 0, 2), (fr, 1, 2)):
        arrived(ref.at[3 - j], xr.at[i, j])

    def total(i, carry):
        part = pl.ds(pl.multiple_of(i * 64, 64), 64)
        below = pl.ds(pl.multiple_of(MID + i * 64, 64), 64)
        sb[part, :] = (
            terms_ref[part, rows_of(q0)].astype(F32) + fl[1, part, :].astype(F32) + fr[2, part, :].astype(F32)
        ).astype(BF16)
        sb[below, :] = (
            terms_ref[below, rows_of(q0)].astype(F32) + fr[1, part, :].astype(F32) + fl[2, part, :].astype(F32)
        ).astype(BF16)
        return carry

    lax.fori_loop(0, MID // 64, total, 0)
    last = []
    for k, (rd, cd, own) in enumerate(spread_sources()):
        piece = sb.at[pl.ds(k * FEAT, FEAT), :]
        at = zl * 2 + y // 2
        cp = remote(piece, ib.at[at], s2s.at[k], s2r.at[at], rd, cd)
        here = pltpu.make_async_copy(piece, ib.at[at], s2r.at[at])

        @pl.when(jnp.logical_not(own))
        def _():
            cp.start()

        @pl.when(own)
        def _():
            here.start()

        last.append((cp, own))

    froms = ((r, o), (r ^ 2, h), (r ^ 2, o))
    for k in range(3):
        at = 2 * froms[k][0] + froms[k][1]
        ref = ub.at[at]
        arrived(ref, cr.at[k])
        if k == 0:
            send(ref, ref, cs.at[2], cr.at[2], r ^ 2, c)
        send(ref, ref, ds_.at[k], dr.at[k], r ^ 1, c)
        update_rows(*froms[k])
        if k < 2:
            rs, hs = froms[k][0] ^ 1, froms[k][1]
            arrived(ub.at[2 * rs + hs], dr.at[k])
            update_rows(rs, hs)
        if k == 1:
            for j in range(4):
                arrived(ib.at[j], s2r.at[j])
            ig_ref[...] = (
                (ib[0].astype(F32) + ib[1].astype(F32)) + (ib[2].astype(F32) + ib[3].astype(F32))
            ).astype(BF16)
    arrived(ub.at[2 * (r ^ 3) + o], dr.at[2])
    update_rows(r ^ 3, o)

    for cp, own in last:
        @pl.when(jnp.logical_not(own))
        def _():
            cp.wait_send()
    for cp in others:
        cp.wait_send()


def ortho_scatter_call(grad, momentum, terms, weight):
    vm = pl.BlockSpec(memory_space=pltpu.VMEM)
    dma = pltpu.SemaphoreType.DMA
    return pl.pallas_call(
        ortho_scatter_kernel,
        out_shape=(
            jax.ShapeDtypeStruct((BR, BC), F32),
            jax.ShapeDtypeStruct((BR, BC), BF16),
            jax.ShapeDtypeStruct((FEAT, TOK), BF16),
            jax.ShapeDtypeStruct(weight.shape, BF16),
        ),
        in_specs=[vm, vm, vm, pl.BlockSpec(memory_space=pltpu.HBM)],
        out_specs=(vm, vm, vm, vm),
        scratch_shapes=[
            pltpu.VMEM((8, BC), F32),
            pltpu.VMEM((2, BR, BR), BF16),
            pltpu.VMEM((BR, BC), BF16),
            pltpu.VMEM((3, BR // 2, TOK), BF16),
            pltpu.VMEM((3, BR // 2, TOK), BF16),
            pltpu.VMEM((BR, TOK), BF16),
            pltpu.VMEM((4, FEAT, TOK), BF16),
            pltpu.VMEM((8, BR, HALF), BF16),
            dma((2, 3)), dma((2, 3)), dma((3,)), dma((3,)), dma((4,)), dma((4,)),
            dma((4,)), dma((4,)), dma((2,)),
        ],
        compiler_params=pltpu.CompilerParams(
            collective_id=1, has_side_effects=True, vmem_limit_bytes=34_000_000
        ),
        cost_estimate=pl.CostEstimate(flops=7_000_000_000, bytes_accessed=20_000_000, transcendentals=0),
        name="ortho_scatter",
    )(grad, momentum, terms, weight)


def body(tokens, cotangent, weight, momentum):
    grad, terms = gather_call(tokens.T, cotangent, weight)
    new_momentum, xmat, input_grad, new_weight = ortho_scatter_call(grad, momentum[0], terms, weight)
    update = 32.0 * xmat.astype(F32)
    return new_weight, input_grad.T, new_momentum[None], update[None]


def solution(mesh):
    in_specs = (P("rows", "cols"), P("rows", "cols"), P(None, "cols"), P(("rows", "cols"), None, None))
    out_specs = (
        P(None, "cols"),
        P("rows", "cols"),
        P(("rows", "cols"), None, None),
        P(("rows", "cols"), None, None),
    )
    return jax.shard_map(body, mesh=mesh, in_specs=in_specs, out_specs=out_specs, check_vma=False)
```

time: 176 us -> 158 us (0.90)
  the two profiles are of different devices: /device:TPU:0 before, /device:TPU:67 now
where the time goes in v2:
time: 158 us; the launch traced here: 157 us
  Pallas kernels  144 us (91%)
  local copies, waits for them, and re-layouts  10.6 us (7%)
  other arithmetic  2.09 us (1%)
    pallas_call x1, Pallas kernels, ortho_scatter_call(): pl.pallas_call(ortho_scatter_kernel, out_shape=(jax.ShapeDtypeStruct((BR,...  86.2 us
    pallas_call x1, Pallas kernels, gather_call(): pl.pallas_call(gather_kernel, out_shape=(jax.ShapeDtypeStruct((BR, BC), F...  57.8 us
    unnamed x13, local copies, waits for them, and re-layouts  10.6 us

profile of v2, /device:TPU:67, one launch (start us, length us, event | category | flops | bytes accessed | tf_op | source)
XLA Modules:
  0.0 157.3 jit_solution(2927146447066081348)
XLA Ops:
  0.6 0.0 copy-start.1
  0.6 1.0 copy-done.1
  1.7 0.0 copy-start.2
  1.7 0.9 copy-done.2
  2.6 0.0 copy-start
  2.6 57.8 %gather_dots.1 = (f32[768,1024]{1,0:T(8,128)S(1)}, bf16[768,2048]{1,0:T(8,128)(2,1)S(1)}) custom-call(bf16[192,512]{1,0:T(8,128)(2,1)S(1)} %bitcast.9, bf16[512,512]{1,0:T(8,128)(2,1)S(1)} %copy-done.1, bf16[6144,512]{1,0:T(8,128)(2,1)} %w_ref.3), custom_call_target="tpu_custom_call" | custom-call | flops 7000000000 | bytes 20000000 | tf_op jit(solution)/shard_map/gather_dots/pallas_call | solution.py:259
  60.4 0.0 copy-start.3
  60.5 1.7 %copy-done.3 = bf16[768,2048]{1,0:T(8,128)(2,1)} copy-done((bf16[768,2048]{1,0:T(8,128)(2,1)}, bf16[768,2048]{1,0:T(8,128)(2,1)S(1)}, u32[]{:S(2)}) %copy-start.3) | copy-done | bytes 3145752
  62.1 0.0 copy-done
  62.1 0.0 copy-start.4
  62.1 1.9 %copy-done.4 = bf16[768,2048]{1,0:T(8,128)(2,1)S(1)} copy-done((bf16[768,2048]{1,0:T(8,128)(2,1)S(1)}, bf16[768,2048]{1,0:T(8,128)(2,1)}, u32[]{:S(2)}) %copy-start.4) | copy-done | bytes 3145752
  64.0 86.2 %ortho_scatter.1 = (f32[768,1024]{1,0:T(8,128)S(1)}, bf16[768,1024]{1,0:T(8,128)(2,1)S(1)}, bf16[192,512]{1,0:T(8,128)(2,1)S(1)}, bf16[6144,512]{1,0:T(8,128)(2,1)S(1)}) custom-call(f32[768,1024]{1,0:T(8,128)S(1)} %get-tuple-element.10.grad_ref, f32[768,1024]{1,0:T(8,128)S(1)} %bitcast.8, bf16[768,2048]{1,0:T(8,128)(2,1)S(1)} %copy-done.4, ...), custom_call_target="tpu_custom_call" | custom-call | flops 7000000000 | bytes 20000000 | tf_op jit(solution)/shard_map/ortho_scatter/pallas_call | solution.py:455
  150.2 2.1 %multiply_bitcast_fusion = f32[1,768,1024]{2,1,0:T(8,128)} fusion(bf16[768,1024]{1,0:T(8,128)(2,1)S(1)} %get-tuple-element.15), kind=kLoop, calls=%fused_computation | loop fusion | flops 1572864 | bytes 4718592 | tf_op jit(solution)/shard_map/broadcast_in_dim | solution.py:489
  152.3 2.7 %copy.11 = bf16[6144,512]{1,0:T(8,128)(2,1)} copy(bf16[6144,512]{1,0:T(8,128)(2,1)S(1)} %get-tuple-element.20) | data formatting | bytes 12582912
  155.0 0.7 copy.12
  155.7 1.7 %copy.13 = f32[1,768,1024]{2,1,0:T(8,128)} copy(f32[1,768,1024]{2,1,0:T(8,128)S(1)} %bitcast.6) | data formatting | bytes 6291456
Async XLA Ops:
  0.6 1.0 copy-start.1
  1.7 0.9 copy-start.2
  2.6 59.5 %copy-start = (f32[1,768,1024]{2,1,0:T(8,128)S(1)}, f32[1,768,1024]{2,1,0:T(8,128)}, u32[]{:S(2)}) copy-start(f32[1,768,1024]{2,1,0:T(8,128)} %param.7) | copy-start | bytes 9437188
  60.4 1.7 %copy-start.3 = (bf16[768,2048]{1,0:T(8,128)(2,1)}, bf16[768,2048]{1,0:T(8,128)(2,1)S(1)}, u32[]{:S(2)}) copy-start(bf16[768,2048]{1,0:T(8,128)(2,1)S(1)} %get-tuple-element.11.terms_ref) | copy-start | bytes 9437188
  62.1 1.9 %copy-start.4 = (bf16[768,2048]{1,0:T(8,128)(2,1)S(1)}, bf16[768,2048]{1,0:T(8,128)(2,1)}, u32[]{:S(2)}) copy-start(bf16[768,2048]{1,0:T(8,128)(2,1)} %copy-done.3) | copy-start | bytes 9437188

commit v3 on v2

v3 whole, which is shorter than its diff:
```python
import functools

import jax
import jax.numpy as jnp
from jax import lax
from jax.experimental import pallas as pl
from jax.experimental.pallas import tpu as pltpu
from jax.sharding import PartitionSpec as P

NS_STEPS = 2
TOK = 512
FEAT = 192
BR = 768
BC = 1024
HALF = 512
COEF_A = 3.4445
COEF_B = -4.775
COEF_C = 2.0315
BETA = 0.95

MESH = pl.DeviceIdType.MESH
F32 = jnp.float32
BF16 = jnp.bfloat16


def place():
    r = lax.axis_index("rows")
    c = lax.axis_index("cols")
    return r, c, c // 8, (c // 4) % 2, c % 4


def remote(src, dst, send, recv, r, c):
    return pltpu.make_async_remote_copy(
        src_ref=src,
        dst_ref=dst,
        send_sem=send,
        recv_sem=recv,
        device_id=(r, c),
        device_id_type=MESH,
    )


def flip(v):
    return (v % 2) * 2 + v // 2


def group_at(x, r):
    return flip((x + 4 - r) % 4)


def spread_targets():
    r, c, x, zl, y = place()
    out = []
    for zd in range(2):
        for yb in range(2):
            col = ((x + flip(r)) % 4) * 8 + zd * 4 + zl + 2 * yb
            out.append((x, col, (x == r) & (col == c)))
    return out


def spread_sources():
    r, c, x, zl, y = place()
    group = group_at(x, r)
    base = r * 8 + (y % 2) * 4
    return [(group, base + k, (group == r) & (base + k == c)) for k in range(4)]


def x_neighbours():
    r, c, x, zl, y = place()
    low = c % 8
    return ((x + 3) % 4) * 8 + low, ((x + 1) % 4) * 8 + low


def signal_unless(flag, barrier, r, c):
    @pl.when(jnp.logical_not(flag))
    def _():
        pl.semaphore_signal(barrier, inc=1, device_id=(r, c), device_id_type=MESH)


def entry_barrier():
    r, c, x, zl, y = place()
    left, right = x_neighbours()
    barrier = pltpu.get_barrier_semaphore()
    for rd, cd in ((r, left), (r, right), (r ^ 2, c), (r, c ^ 1), (r ^ 1, c)):
        pl.semaphore_signal(barrier, inc=1, device_id=(rd, cd), device_id_type=MESH)
    targets, sources = spread_targets(), spread_sources()
    for rd, cd, own in targets + sources:
        signal_unless(own, barrier, rd, cd)
    own_count = sum(jnp.where(own, 1, 0) for _, _, own in targets + sources)
    pl.semaphore_wait(barrier, 13 - own_count)


def rows_of(group):
    return pl.ds(pl.multiple_of(group * TOK, TOK), TOK)


def half_of(which):
    return pl.ds(pl.multiple_of(which * HALF, HALF), HALF)


def arrived(ref, sem):
    pltpu.make_async_copy(ref, ref, sem).wait()


def tiles(step, rows=256):
    def run(i, carry):
        step(pl.ds(pl.multiple_of(i * rows, rows), rows))
        return carry

    lax.fori_loop(0, BR // rows, run, 0)


CH = 3
CR = BR // CH


def chunk(t):
    return pl.ds(t * CR, CR)


def step_kernel(
    tok_ref, cot_ref, w_ref, mom_ref, newm_ref, x_ref, ig_ref, neww_ref,
    tokv, tokg, cotg, wcat, tacc, terms, sq, ab, xb, fl, fr, sb, ib, ub,
    s1s, s1r, xs, xr, cs, cr, ds_, dr, ws, wr, ls,
    ps, pr, us, ur, vs, vr, s2s, s2r,
):
    r, c, x, zl, y = place()
    h = c % 2
    o = 1 - h
    left, right = x_neighbours()
    mine = cotg.at[rows_of(r), half_of(h)]
    own_tok = pltpu.make_async_copy(tok_ref, tokv, ls.at[0])
    own_cot = pltpu.make_async_copy(cot_ref, mine, ls.at[1])
    own_w = pltpu.make_async_copy(
        w_ref.at[pl.ds(pl.multiple_of((2 * r + h) * BR, BR), BR), :], wcat.at[:, half_of(h)], ls.at[2]
    )
    load_m = pltpu.make_async_copy(mom_ref, newm_ref, ls.at[3])
    load_w = pltpu.make_async_copy(w_ref, neww_ref, ls.at[4])
    for cp in (own_tok, own_cot, own_w, load_m, load_w):
        cp.start()
    entry_barrier()
    own_tok.wait()

    def send_spread(pairs, make):
        out = []
        for k, (rd, cd, own) in enumerate(pairs):
            cp, here = make(k, rd, cd)

            @pl.when(jnp.logical_not(own))
            def _():
                cp.start()

            @pl.when(own)
            def _():
                here.start()

            out.append((cp, own))
        return out

    def spread_tokens(k, rd, cd):
        dst = tokg.at[pl.ds(pl.multiple_of(y * FEAT, FEAT), FEAT), rows_of(r)]
        return remote(tokv, dst, s1s.at[k], s1r.at[y], rd, cd), pltpu.make_async_copy(tokv, dst, s1r.at[y])

    spreads = send_spread(spread_targets(), spread_tokens)

    own_cot.wait()
    others = []

    def send(src, dst, ss, rs, rd, cd):
        cp = remote(src, dst, ss, rs, rd, cd)
        cp.start()
        others.append(cp)

    send(mine, mine, cs.at[0], cr.at[0], r, c ^ 1)
    send(mine, mine, cs.at[1], cr.at[1], r ^ 2, c)
    send(mine, mine, ds_.at[3], dr.at[3], r ^ 1, c)

    send(
        w_ref.at[pl.ds(pl.multiple_of((2 * r + o) * BR, BR), BR), :],
        wcat.at[:, half_of(h)], ws.at[0], wr.at[0], r, c ^ 1,
    )

    q0, ql, qr, q2 = (group_at((x + k) % 4, r) for k in (0, 3, 1, 2))
    for k in range(4):
        piece = tokg.at[pl.ds(k * FEAT, FEAT), rows_of(q0)]
        arrived(piece, s1r.at[k])
        send(piece, piece, xs.at[0, k], xr.at[0, k], r, left)
        send(piece, piece, xs.at[1, k], xr.at[1, k], r, right)

    froms = ((r, o), (r ^ 2, h), (r ^ 2, o))

    def pass_on(k):
        ref = cotg.at[rows_of(froms[k][0]), half_of(froms[k][1])]
        arrived(ref, cr.at[k])
        if k == 0:
            send(ref, ref, cs.at[2], cr.at[2], r ^ 2, c)
        send(ref, ref, ds_.at[k], dr.at[k], r ^ 1, c)

    pass_on(0)
    pass_on(1)

    for k in range(2):
        ref = tokg.at[pl.ds(k * FEAT, FEAT), rows_of(ql)]
        arrived(ref, xr.at[1, k])
        send(ref, ref, xs.at[2, k], xr.at[2, k], r, right)
        ref = tokg.at[pl.ds((k + 2) * FEAT, FEAT), rows_of(qr)]
        arrived(ref, xr.at[0, k + 2])
        send(ref, ref, xs.at[2, k + 2], xr.at[2, k + 2], r, left)

    def from_core(k, rs, hs):
        arrived(cotg.at[rows_of(rs), half_of(hs)], dr.at[k])

    own_w.wait()
    from_core(3, r ^ 1, h)
    from_core(1, r ^ 3, h)
    nt = (((1,), (1,)), ((), ()))

    def terms_half(which, group, first):
        def tile(rows):
            part = lax.dot_general(
                wcat[rows, half_of(which)], cotg[rows_of(group), half_of(which)], nt,
                preferred_element_type=F32,
            )
            if first:
                tacc[rows, rows_of(group)] = part
            else:
                terms[rows, rows_of(group)] = (tacc[rows, rows_of(group)] + part).astype(BF16)

        tiles(tile)

    def all_first(group, carry):
        terms_half(h, group, True)
        return carry

    lax.fori_loop(0, 4, all_first, 0)
    pass_on(2)
    from_core(0, r ^ 1, o)
    from_core(2, r ^ 3, o)

    load_m.wait()
    sq[...] = jnp.zeros_like(sq)

    def grad_step(group, first=False, last=False):
        def tile(rows):
            part = jnp.dot(tokg[rows, rows_of(group)], cotg[rows_of(group), :], preferred_element_type=F32)
            old = newm_ref[rows, :]
            new = (BETA * old if first else old) + part
            newm_ref[rows, :] = new
            if last:
                sq[...] += jnp.sum((new * new).reshape(-1, 8, BC), axis=0)

        tiles(tile)

    grad_step(q0, first=True)
    for k in range(2):
        arrived(tokg.at[pl.ds(k * FEAT, FEAT), rows_of(qr)], xr.at[0, k])
        arrived(tokg.at[pl.ds((k + 2) * FEAT, FEAT), rows_of(ql)], xr.at[1, k + 2])
    grad_step(ql)
    grad_step(qr)
    arrived(wcat.at[:, half_of(o)], wr.at[0])

    MID = BR // 2
    top, low = pl.ds(0, MID), pl.ds(MID, MID)
    terms_half(o, q2, False)
    terms_half(o, qr, False)
    send(terms.at[top, rows_of(q2)], fl.at[0], ps.at[0, 0], pr.at[0, 0], r, right)
    send(terms.at[low, rows_of(q2)], fr.at[0], ps.at[1, 0], pr.at[1, 0], r, left)
    terms_half(o, ql, False)
    send(terms.at[low, rows_of(qr)], fl.at[2], ps.at[0, 1], pr.at[0, 1], r, right)
    terms_half(o, q0, False)
    send(terms.at[top, rows_of(ql)], fr.at[2], ps.at[1, 1], pr.at[1, 1], r, left)
    for k in range(4):
        arrived(tokg.at[pl.ds(k * FEAT, FEAT), rows_of(q2)], xr.at[2, k])
    grad_step(q2, last=True)

    def join(src, base, group):
        def step(i, carry):
            part = pl.ds(pl.multiple_of(i * 64, 64), 64)
            here = pl.ds(pl.multiple_of(base + i * 64, 64), 64)
            src[0, part, :] = (
                src[0, part, :].astype(F32) + terms[here, rows_of(group)].astype(F32)
            ).astype(BF16)
            return carry

        lax.fori_loop(0, MID // 64, step, 0)

    def join_both():
        arrived(fl.at[0], pr.at[0, 0])
        arrived(fr.at[0], pr.at[1, 0])
        join(fl, 0, qr)
        join(fr, MID, ql)
        send(fl.at[0], fl.at[1], ps.at[0, 2], pr.at[0, 2], r, right)
        send(fr.at[0], fr.at[1], ps.at[1, 2], pr.at[1, 2], r, left)

    inverse = 1.0 / (jnp.sqrt(jnp.sum(sq[...])) + 1e-07)

    def scaled(rows):
        x_ref[rows, :] = (newm_ref[rows, :] * inverse).astype(BF16)

    tiles(scaled, 64)

    def send_update(t):
        rows = chunk(t)
        slot = ub.at[2 * r + h, rows, :]
        send(x_ref.at[rows, half_of(o)], slot, us.at[0, t], ur.at[0, t], r, c ^ 1)
        send(x_ref.at[rows, half_of(h)], slot, us.at[1, t], ur.at[1, t], r ^ 2, c)
        send(x_ref.at[rows, half_of(h)], slot, vs.at[3, t], vr.at[3, t], r ^ 1, c)

    def update_rows(rs, hs, t, own=False):
        at = 2 * rs + hs

        def step(i, carry):
            part = pl.ds(pl.multiple_of(t * CR + i * 64, 64), 64)
            here = pl.ds(pl.multiple_of(at * BR + t * CR + i * 64, 64), 64)
            new = x_ref[part, half_of(h)] if own else ub[at, part, :]
            neww_ref[here, :] = (neww_ref[here, :].astype(F32) - 8.0 * new.astype(F32)).astype(BF16)
            return carry

        lax.fori_loop(0, CR // 64, step, 0)

    load_w.wait()
    src, dst = x_ref, xb
    for step in range(NS_STEPS):
        def gram(rows):
            ab[0, rows, :] = lax.dot_general(src[rows, :], src[...], nt, preferred_element_type=F32).astype(BF16)

        def poly(rows):
            a = ab[0, rows, :]
            aa = jnp.dot(a, ab[0], preferred_element_type=F32)
            ab[1, rows, :] = (COEF_B * a.astype(F32) + COEF_C * aa).astype(BF16)

        def apply(rows):
            bx = jnp.dot(ab[1, rows, :], src[...], preferred_element_type=F32)
            dst[rows, :] = (COEF_A * src[rows, :].astype(F32) + bx).astype(BF16)

        tiles(gram)
        tiles(poly)
        if step == 0:
            tiles(apply)
            join_both()
        else:
            apply(chunk(0))
            apply(chunk(1))
            send_update(0)
            apply(chunk(2))
            send_update(1)
            update_rows(r, h, 0, own=True)
            send_update(2)
        src, dst = dst, src

    update_rows(r, h, 1, own=True)
    update_rows(r, h, 2, own=True)

    for ref, i, j in ((fl, 0, 1), (fr, 1, 1), (fl, 0, 2), (fr, 1, 2)):
        arrived(ref.at[3 - j], pr.at[i, j])

    def total(i, carry):
        part = pl.ds(pl.multiple_of(i * 64, 64), 64)
        below = pl.ds(pl.multiple_of(MID + i * 64, 64), 64)
        sb[part, :] = (
            terms[part, rows_of(q0)].astype(F32) + fl[1, part, :].astype(F32) + fr[2, part, :].astype(F32)
        ).astype(BF16)
        sb[below, :] = (
            terms[below, rows_of(q0)].astype(F32) + fr[1, part, :].astype(F32) + fl[2, part, :].astype(F32)
        ).astype(BF16)
        return carry

    lax.fori_loop(0, MID // 64, total, 0)

    def spread_sums(k, rd, cd):
        piece = sb.at[pl.ds(k * FEAT, FEAT), :]
        at = zl * 2 + y // 2
        return (
            remote(piece, ib.at[at], s2s.at[k], s2r.at[at], rd, cd),
            pltpu.make_async_copy(piece, ib.at[at], s2r.at[at]),
        )

    def relay(k, t):
        ref = ub.at[2 * froms[k][0] + froms[k][1], chunk(t), :]
        arrived(ref, ur.at[k, t])
        if k == 0:
            send(ref, ref, us.at[2, t], ur.at[2, t], r ^ 2, c)
        send(ref, ref, vs.at[k, t], vr.at[k, t], r ^ 1, c)

    def core_rows(k, t):
        rs, hs = (froms[k][0] ^ 1, froms[k][1]) if k < 3 else (r ^ 1, h)
        arrived(ub.at[2 * rs + hs, chunk(t), :], vr.at[k, t])
        update_rows(rs, hs, t)

    spreads += send_spread(spread_sources(), spread_sums)
    for t in range(CH):
        relay(0, t)
        relay(1, t)
    for t in range(CH):
        core_rows(3, t)
        update_rows(*froms[0], t)
        update_rows(*froms[1], t)
        core_rows(0, t)
        core_rows(1, t)
    for j in range(4):
        arrived(ib.at[j], s2r.at[j])
    ig_ref[...] = (
        (ib[0].astype(F32) + ib[1].astype(F32)) + (ib[2].astype(F32) + ib[3].astype(F32))
    ).astype(BF16)
    for t in range(CH):
        relay(2, t)
        update_rows(*froms[2], t)
        core_rows(2, t)

    for cp, own in spreads:
        @pl.when(jnp.logical_not(own))
        def _():
            cp.wait_send()
    for cp in others:
        cp.wait_send()


def step_call(tok, cot, weight, momentum):
    hbm = pl.BlockSpec(memory_space=pltpu.HBM)
    vm = pl.BlockSpec(memory_space=pltpu.VMEM)
    dma = pltpu.SemaphoreType.DMA
    return pl.pallas_call(
        step_kernel,
        out_shape=(
            jax.ShapeDtypeStruct((BR, BC), F32),
            jax.ShapeDtypeStruct((BR, BC), BF16),
            jax.ShapeDtypeStruct((FEAT, TOK), BF16),
            jax.ShapeDtypeStruct(weight.shape, BF16),
        ),
        in_specs=[hbm, hbm, hbm, hbm],
        out_specs=(vm, vm, vm, vm),
        scratch_shapes=[
            pltpu.VMEM((FEAT, TOK), BF16),
            pltpu.VMEM((BR, 4 * TOK), BF16),
            pltpu.VMEM((4 * TOK, BC), BF16),
            pltpu.VMEM((BR, BC), BF16),
            pltpu.VMEM((BR, 4 * TOK), F32),
            pltpu.VMEM((BR, 4 * TOK), BF16),
            pltpu.VMEM((8, BC), F32),
            pltpu.VMEM((2, BR, BR), BF16),
            pltpu.VMEM((BR, BC), BF16),
            pltpu.VMEM((3, BR // 2, TOK), BF16),
            pltpu.VMEM((3, BR // 2, TOK), BF16),
            pltpu.VMEM((BR, TOK), BF16),
            pltpu.VMEM((4, FEAT, TOK), BF16),
            pltpu.VMEM((8, BR, HALF), BF16),
            dma((4,)), dma((4,)), dma((3, 4)), dma((3, 4)), dma((3,)), dma((3,)),
            dma((4,)), dma((4,)), dma((1,)), dma((1,)), dma((5,)),
            dma((2, 3)), dma((2, 3)), dma((3, CH)), dma((3, CH)), dma((4, CH)), dma((4, CH)),
            dma((4,)), dma((4,)),
        ],
        compiler_params=pltpu.CompilerParams(
            collective_id=0, has_side_effects=True, vmem_limit_bytes=40_000_000
        ),
        cost_estimate=pl.CostEstimate(flops=14_000_000_000, bytes_accessed=20_000_000, transcendentals=0),
        name="step",
    )(tok, cot, weight, momentum)


def write_kernel(newm_ref, x_ref, ig_ref, neww_ref, newm_out, upd_out, ig_out, neww_out, buf, sem):
    copies = [
        pltpu.make_async_copy(neww_ref, neww_out, sem.at[0]),
        pltpu.make_async_copy(newm_ref, newm_out, sem.at[1]),
        pltpu.make_async_copy(ig_ref, ig_out, sem.at[2]),
    ]
    for cp in copies:
        cp.start()
    for t in range(CH):
        buf[chunk(t), :] = 32.0 * x_ref[chunk(t), :].astype(F32)
        cp = pltpu.make_async_copy(buf.at[chunk(t), :], upd_out.at[chunk(t), :], sem.at[3 + t])
        cp.start()
        copies.append(cp)
    for cp in copies:
        cp.wait()


def write_call(newm, xmat, ig, neww):
    hbm = pl.BlockSpec(memory_space=pltpu.HBM)
    vm = pl.BlockSpec(memory_space=pltpu.VMEM)
    return pl.pallas_call(
        write_kernel,
        out_shape=(
            jax.ShapeDtypeStruct(newm.shape, F32),
            jax.ShapeDtypeStruct(xmat.shape, F32),
            jax.ShapeDtypeStruct(ig.shape, BF16),
            jax.ShapeDtypeStruct(neww.shape, BF16),
        ),
        in_specs=[vm, vm, vm, vm],
        out_specs=(hbm, hbm, hbm, hbm),
        scratch_shapes=[pltpu.VMEM((BR, BC), F32), pltpu.SemaphoreType.DMA((3 + CH,))],
        compiler_params=pltpu.CompilerParams(vmem_limit_bytes=20_000_000),
        cost_estimate=pl.CostEstimate(flops=1_000_000, bytes_accessed=13_000_000, transcendentals=0),
        name="write_out",
    )(newm, xmat, ig, neww)


def body(tokens, cotangent, weight, momentum):
    pin = lambda a: pltpu.with_memory_space_constraint(a, pltpu.HBM)
    results = step_call(pin(tokens.T), pin(cotangent), pin(weight), pin(momentum[0]))
    new_momentum, update, input_grad, new_weight = write_call(*results)
    return new_weight, input_grad.T, new_momentum[None], update[None]


def solution(mesh):
    in_specs = (P("rows", "cols"), P("rows", "cols"), P(None, "cols"), P(("rows", "cols"), None, None))
    out_specs = (
        P(None, "cols"),
        P("rows", "cols"),
        P(("rows", "cols"), None, None),
        P(("rows", "cols"), None, None),
    )
    return jax.shard_map(body, mesh=mesh, in_specs=in_specs, out_specs=out_specs, check_vma=False)
```

time: 158 us -> 139 us (0.88)
  the two profiles are of different devices: /device:TPU:67 before, /device:TPU:55 now
where the time goes in v3:
time: 139 us; the launch traced here: 138 us
  Pallas kernels  138 us (99%)
    pallas_call x1, Pallas kernels, step_call(): pl.pallas_call(step_kernel, out_shape=(jax.ShapeDtypeStruct((BR, BC), F32...  133 us
    pallas_call x1, Pallas kernels, write_call(): pl.pallas_call(write_kernel, out_shape=(jax.ShapeDtypeStruct(newm.shape,...  4.73 us

profile of v3, /device:TPU:55, one launch (start us, length us, event | category | flops | bytes accessed | tf_op | source)
XLA Modules:
  0.0 138.5 jit_solution(15480783182173894452)
XLA Ops:
  0.6 133.1 %step.1 = (f32[768,1024]{1,0:T(8,128)S(1)}, bf16[768,1024]{1,0:T(8,128)(2,1)S(1)}, bf16[192,512]{1,0:T(8,128)(2,1)S(1)}, bf16[6144,512]{1,0:T(8,128)(2,1)S(1)}) custom-call(bf16[192,512]{1,0:T(8,128)(2,1)} %bitcast.8, bf16[512,512]{1,0:T(8,128)(2,1)} %cot_ref.1, bf16[6144,512]{1,0:T(8,128)(2,1)} %w_ref.1, f32[768,1024]{1,0:T(8,128)} %bitcast.5), custom_call_target="tpu_custom_call" | custom-call | flops 14000000000 | bytes 20000000 | tf_op jit(solution)/shard_map/step/pallas_call | solution.py:422
  133.8 4.7 %write_out.1 = (f32[768,1024]{1,0:T(8,128)}, f32[768,1024]{1,0:T(8,128)}, bf16[192,512]{1,0:T(8,128)(2,1)}, bf16[6144,512]{1,0:T(8,128)(2,1)}) custom-call(f32[768,1024]{1,0:T(8,128)S(1)} %get-tuple-element.12.newm_ref, bf16[768,1024]{1,0:T(8,128)(2,1)S(1)} %get-tuple-element.13.x_ref, bf16[192,512]{1,0:T(8,128)(2,1)S(1)} %get-tuple-element.14.ig_ref, ...), custom_call_target="tpu_custom_call" | custom-call | flops 1000000 | bytes 13000000 | tf_op jit(solution)/shard_map/write_out/pallas_call | solution.py:480

commit v4 on v3

--- a/solution.py
+++ b/solution.py
@@ -50,19 +50,15 @@
 
 def spread_targets():
     r, c, x, zl, y = place()
-    out = []
-    for zd in range(2):
-        for yb in range(2):
-            col = ((x + flip(r)) % 4) * 8 + zd * 4 + zl + 2 * yb
-            out.append((x, col, (x == r) & (col == c)))
-    return out
+    base = ((x + flip(r)) % 4) * 8 + zl + 2 * (y // 2)
+    return [(x, base + 4 * k, (x == r) & (base + 4 * k == c)) for k in range(2)]
 
 
 def spread_sources():
     r, c, x, zl, y = place()
     group = group_at(x, r)
-    base = r * 8 + (y % 2) * 4
-    return [(group, base + k, (group == r) & (base + k == c)) for k in range(4)]
+    base = r * 8 + (y % 2) * 4 + 2 * (y // 2)
+    return [(group, base + k, (group == r) & (base + k == c)) for k in range(2)]
 
 
 def x_neighbours():
@@ -81,13 +77,13 @@
     r, c, x, zl, y = place()
     left, right = x_neighbours()
     barrier = pltpu.get_barrier_semaphore()
-    for rd, cd in ((r, left), (r, right), (r ^ 2, c), (r, c ^ 1), (r ^ 1, c)):
+    for rd, cd in ((r, left), (r, right), (r ^ 2, c), (r, c ^ 1), (r, c ^ 2), (r ^ 1, c)):
         pl.semaphore_signal(barrier, inc=1, device_id=(rd, cd), device_id_type=MESH)
     targets, sources = spread_targets(), spread_sources()
     for rd, cd, own in targets + sources:
         signal_unless(own, barrier, rd, cd)
     own_count = sum(jnp.where(own, 1, 0) for _, _, own in targets + sources)
-    pl.semaphore_wait(barrier, 13 - own_count)
+    pl.semaphore_wait(barrier, 10 - own_count)
 
 
 def rows_of(group):
@@ -120,7 +116,7 @@
 
 def step_kernel(
     tok_ref, cot_ref, w_ref, mom_ref, newm_ref, x_ref, ig_ref, neww_ref,
-    tokv, tokg, cotg, wcat, tacc, terms, sq, ab, xb, fl, fr, sb, ib, ub,
+    tokv, tokg, cotg, wcat, tacc, terms, sq, ab, xb, fl, fr, sb, sp, ib, ub,
     s1s, s1r, xs, xr, cs, cr, ds_, dr, ws, wr, ls,
     ps, pr, us, ur, vs, vr, s2s, s2r,
 ):
@@ -159,7 +155,8 @@
 
     def spread_tokens(k, rd, cd):
         dst = tokg.at[pl.ds(pl.multiple_of(y * FEAT, FEAT), FEAT), rows_of(r)]
-        return remote(tokv, dst, s1s.at[k], s1r.at[y], rd, cd), pltpu.make_async_copy(tokv, dst, s1r.at[y])
+        got = s1r.at[y % 2]
+        return remote(tokv, dst, s1s.at[k], got, rd, cd), pltpu.make_async_copy(tokv, dst, got)
 
     spreads = send_spread(spread_targets(), spread_tokens)
 
@@ -175,17 +172,28 @@
     send(mine, mine, cs.at[1], cr.at[1], r ^ 2, c)
     send(mine, mine, ds_.at[3], dr.at[3], r ^ 1, c)
 
+    q0, ql, qr, q2 = (group_at((x + k) % 4, r) for k in (0, 3, 1, 2))
+    yb = y // 2
+
+    def piece(j, group):
+        at = (2 * yb + j) % 4
+        return tokg.at[pl.ds(pl.multiple_of(at * FEAT, FEAT), FEAT), rows_of(group)]
+
+    def round_x(j):
+        ref = piece(j, q0)
+        arrived(ref, s1r.at[j])
+        if j < 2:
+            send(ref, ref, s1s.at[2 + j], s1r.at[2 + j], r, c ^ 2)
+        send(ref, ref, xs.at[0, j], xr.at[0, j], r, left)
+        send(ref, ref, xs.at[1, j], xr.at[1, j], r, right)
+
+    round_x(0)
+    round_x(1)
+
     send(
         w_ref.at[pl.ds(pl.multiple_of((2 * r + o) * BR, BR), BR), :],
         wcat.at[:, half_of(h)], ws.at[0], wr.at[0], r, c ^ 1,
     )
-
-    q0, ql, qr, q2 = (group_at((x + k) % 4, r) for k in (0, 3, 1, 2))
-    for k in range(4):
-        piece = tokg.at[pl.ds(k * FEAT, FEAT), rows_of(q0)]
-        arrived(piece, s1r.at[k])
-        send(piece, piece, xs.at[0, k], xr.at[0, k], r, left)
-        send(piece, piece, xs.at[1, k], xr.at[1, k], r, right)
 
     froms = ((r, o), (r ^ 2, h), (r ^ 2, o))
 
@@ -197,15 +205,15 @@
         send(ref, ref, ds_.at[k], dr.at[k], r ^ 1, c)
 
     pass_on(0)
+    round_x(2)
+    round_x(3)
     pass_on(1)
 
-    for k in range(2):
-        ref = tokg.at[pl.ds(k * FEAT, FEAT), rows_of(ql)]
-        arrived(ref, xr.at[1, k])
-        send(ref, ref, xs.at[2, k], xr.at[2, k], r, right)
-        ref = tokg.at[pl.ds((k + 2) * FEAT, FEAT), rows_of(qr)]
-        arrived(ref, xr.at[0, k + 2])
-        send(ref, ref, xs.at[2, k + 2], xr.at[2, k + 2], r, left)
+    for j in range(4):
+        came, group, to = ((1, ql, right), (0, qr, left))[j % 2]
+        ref = piece(j, group)
+        arrived(ref, xr.at[came, j])
+        send(ref, ref, xs.at[2, j], xr.at[2, j], r, to)
 
     def from_core(k, rs, hs):
         arrived(cotg.at[rows_of(rs), half_of(hs)], dr.at[k])
@@ -252,26 +260,17 @@
         tiles(tile)
 
     grad_step(q0, first=True)
-    for k in range(2):
-        arrived(tokg.at[pl.ds(k * FEAT, FEAT), rows_of(qr)], xr.at[0, k])
-        arrived(tokg.at[pl.ds((k + 2) * FEAT, FEAT), rows_of(ql)], xr.at[1, k + 2])
+    for j in range(4):
+        came, group = ((0, qr), (1, ql))[j % 2]
+        arrived(piece(j, group), xr.at[came, j])
     grad_step(ql)
     grad_step(qr)
-    arrived(wcat.at[:, half_of(o)], wr.at[0])
+    for j in range(4):
+        arrived(piece(j, q2), xr.at[2, j])
+    grad_step(q2, last=True)
 
     MID = BR // 2
     top, low = pl.ds(0, MID), pl.ds(MID, MID)
-    terms_half(o, q2, False)
-    terms_half(o, qr, False)
-    send(terms.at[top, rows_of(q2)], fl.at[0], ps.at[0, 0], pr.at[0, 0], r, right)
-    send(terms.at[low, rows_of(q2)], fr.at[0], ps.at[1, 0], pr.at[1, 0], r, left)
-    terms_half(o, ql, False)
-    send(terms.at[low, rows_of(qr)], fl.at[2], ps.at[0, 1], pr.at[0, 1], r, right)
-    terms_half(o, q0, False)
-    send(terms.at[top, rows_of(ql)], fr.at[2], ps.at[1, 1], pr.at[1, 1], r, left)
-    for k in range(4):
-        arrived(tokg.at[pl.ds(k * FEAT, FEAT), rows_of(q2)], xr.at[2, k])
-    grad_step(q2, last=True)
 
     def join(src, base, group):
         def step(i, carry):
@@ -299,6 +298,17 @@
 
     tiles(scaled, 64)
 
+    def start_sums():
+        arrived(wcat.at[:, half_of(o)], wr.at[0])
+        terms_half(o, q2, False)
+        terms_half(o, qr, False)
+        send(terms.at[top, rows_of(q2)], fl.at[0], ps.at[0, 0], pr.at[0, 0], r, right)
+        send(terms.at[low, rows_of(q2)], fr.at[0], ps.at[1, 0], pr.at[1, 0], r, left)
+        terms_half(o, ql, False)
+        send(terms.at[low, rows_of(qr)], fl.at[2], ps.at[0, 1], pr.at[0, 1], r, right)
+        terms_half(o, q0, False)
+        send(terms.at[top, rows_of(ql)], fr.at[2], ps.at[1, 1], pr.at[1, 1], r, left)
+
     def send_update(t):
         rows = chunk(t)
         slot = ub.at[2 * r + h, rows, :]
@@ -336,8 +346,8 @@
         tiles(gram)
         tiles(poly)
         if step == 0:
+            start_sums()
             tiles(apply)
-            join_both()
         else:
             apply(chunk(0))
             apply(chunk(1))
@@ -350,9 +360,7 @@
 
     update_rows(r, h, 1, own=True)
     update_rows(r, h, 2, own=True)
-
-    for ref, i, j in ((fl, 0, 1), (fr, 1, 1), (fl, 0, 2), (fr, 1, 2)):
-        arrived(ref.at[3 - j], pr.at[i, j])
+    join_both()
 
     def total(i, carry):
         part = pl.ds(pl.multiple_of(i * 64, 64), 64)
@@ -365,15 +373,21 @@
         ).astype(BF16)
         return carry
 
-    lax.fori_loop(0, MID // 64, total, 0)
+    def pieces_of(which):
+        return pl.ds(pl.multiple_of(which * MID, MID), MID)
 
     def spread_sums(k, rd, cd):
-        piece = sb.at[pl.ds(k * FEAT, FEAT), :]
-        at = zl * 2 + y // 2
+        part = sb.at[pl.ds(pl.multiple_of((2 * yb + k) * FEAT, FEAT), FEAT), :]
         return (
-            remote(piece, ib.at[at], s2s.at[k], s2r.at[at], rd, cd),
-            pltpu.make_async_copy(piece, ib.at[at], s2r.at[at]),
+            remote(part, ib.at[zl], s2s.at[k], s2r.at[zl], rd, cd),
+            pltpu.make_async_copy(part, ib.at[zl], s2r.at[zl]),
         )
+
+    def pair_sum(i, carry):
+        part = pl.ds(pl.multiple_of(i * 64, 64), 64)
+        here = pl.ds(pl.multiple_of(yb * MID + i * 64, 64), 64)
+        sb[here, :] = (sb[here, :].astype(F32) + sp[part, :].astype(F32)).astype(BF16)
+        return carry
 
     def relay(k, t):
         ref = ub.at[2 * froms[k][0] + froms[k][1], chunk(t), :]
@@ -387,25 +401,37 @@
         arrived(ub.at[2 * rs + hs, chunk(t), :], vr.at[k, t])
         update_rows(rs, hs, t)
 
-    spreads += send_spread(spread_sources(), spread_sums)
     for t in range(CH):
         relay(0, t)
         relay(1, t)
-    for t in range(CH):
         core_rows(3, t)
         update_rows(*froms[0], t)
         update_rows(*froms[1], t)
+
+    for ref, i, j in ((fl, 0, 1), (fr, 1, 1), (fl, 0, 2), (fr, 1, 2)):
+        arrived(ref.at[3 - j], pr.at[i, j])
+
+    lax.fori_loop(0, MID // 64, total, 0)
+    for t in range(CH):
         core_rows(0, t)
+    send(sb.at[pieces_of(1 - yb), :], sp, s2s.at[2], s2r.at[2], r, c ^ 2)
+    for t in range(CH):
         core_rows(1, t)
-    for j in range(4):
-        arrived(ib.at[j], s2r.at[j])
-    ig_ref[...] = (
-        (ib[0].astype(F32) + ib[1].astype(F32)) + (ib[2].astype(F32) + ib[3].astype(F32))
-    ).astype(BF16)
     for t in range(CH):
         relay(2, t)
         update_rows(*froms[2], t)
-        core_rows(2, t)
+        if t == 0:
+            arrived(sp, s2r.at[2])
+            lax.fori_loop(0, MID // 64, pair_sum, 0)
+            core_rows(2, 0)
+            spreads += send_spread(spread_sources(), spread_sums)
+        elif t == 1:
+            core_rows(2, 1)
+        else:
+            for j in range(2):
+                arrived(ib.at[j], s2r.at[j])
+            ig_ref[...] = (ib[0].astype(F32) + ib[1].astype(F32)).astype(BF16)
+            core_rows(2, 2)
 
     for cp, own in spreads:
         @pl.when(jnp.logical_not(own))
@@ -442,12 +468,13 @@
             pltpu.VMEM((3, BR // 2, TOK), BF16),
             pltpu.VMEM((3, BR // 2, TOK), BF16),
             pltpu.VMEM((BR, TOK), BF16),
-            pltpu.VMEM((4, FEAT, TOK), BF16),
+            pltpu.VMEM((BR // 2, TOK), BF16),
+            pltpu.VMEM((2, FEAT, TOK), BF16),
             pltpu.VMEM((8, BR, HALF), BF16),
             dma((4,)), dma((4,)), dma((3, 4)), dma((3, 4)), dma((3,)), dma((3,)),
             dma((4,)), dma((4,)), dma((1,)), dma((1,)), dma((5,)),
             dma((2, 3)), dma((2, 3)), dma((3, CH)), dma((3, CH)), dma((4, CH)), dma((4, CH)),
-            dma((4,)), dma((4,)),
+            dma((3,)), dma((3,)),
         ],
         compiler_params=pltpu.CompilerParams(
             collective_id=0, has_side_effects=True, vmem_limit_bytes=40_000_000

time: 139 us -> 125 us (0.90)
  the two profiles are of different devices: /device:TPU:55 before, /device:TPU:37 now
where the time goes in v4:
time: 125 us
  Pallas kernels  124 us (99%)
    pallas_call x1, Pallas kernels, step_call(): pl.pallas_call(step_kernel, out_shape=(jax.ShapeDtypeStruct((BR, BC), F32...  120 us
    pallas_call x1, Pallas kernels, write_call(): pl.pallas_call(write_kernel, out_shape=(jax.ShapeDtypeStruct(newm.shape,...  4.73 us

profile of v4, /device:TPU:37, one launch (start us, length us, event | category | flops | bytes accessed | tf_op | source)
XLA Modules:
  0.0 125.0 jit_solution(12961095904195742554)
XLA Ops:
  0.6 119.7 %step.1 = (f32[768,1024]{1,0:T(8,128)S(1)}, bf16[768,1024]{1,0:T(8,128)(2,1)S(1)}, bf16[192,512]{1,0:T(8,128)(2,1)S(1)}, bf16[6144,512]{1,0:T(8,128)(2,1)S(1)}) custom-call(bf16[192,512]{1,0:T(8,128)(2,1)} %bitcast.8, bf16[512,512]{1,0:T(8,128)(2,1)} %cot_ref.1, bf16[6144,512]{1,0:T(8,128)(2,1)} %w_ref.1, f32[768,1024]{1,0:T(8,128)} %bitcast.5), custom_call_target="tpu_custom_call" | custom-call | flops 14000000000 | bytes 20000000 | tf_op jit(solution)/shard_map/step/pallas_call | solution.py:448
  120.3 4.7 %write_out.1 = (f32[768,1024]{1,0:T(8,128)}, f32[768,1024]{1,0:T(8,128)}, bf16[192,512]{1,0:T(8,128)(2,1)}, bf16[6144,512]{1,0:T(8,128)(2,1)}) custom-call(f32[768,1024]{1,0:T(8,128)S(1)} %get-tuple-element.12.newm_ref, bf16[768,1024]{1,0:T(8,128)(2,1)S(1)} %get-tuple-element.13.x_ref, bf16[192,512]{1,0:T(8,128)(2,1)S(1)} %get-tuple-element.14.ig_ref, ...), custom_call_target="tpu_custom_call" | custom-call | flops 1000000 | bytes 13000000 | tf_op jit(solution)/shard_map/write_out/pallas_call | solution.py:507

commit v5 on v4

--- a/solution.py
+++ b/solution.py
@@ -169,7 +169,6 @@
         others.append(cp)
 
     send(mine, mine, cs.at[0], cr.at[0], r, c ^ 1)
-    send(mine, mine, cs.at[1], cr.at[1], r ^ 2, c)
     send(mine, mine, ds_.at[3], dr.at[3], r ^ 1, c)
 
     q0, ql, qr, q2 = (group_at((x + k) % 4, r) for k in (0, 3, 1, 2))
@@ -189,6 +188,7 @@
 
     round_x(0)
     round_x(1)
+    send(mine, mine, cs.at[1], cr.at[1], r ^ 2, c)
 
     send(
         w_ref.at[pl.ds(pl.multiple_of((2 * r + o) * BR, BR), BR), :],
@@ -204,16 +204,18 @@
             send(ref, ref, cs.at[2], cr.at[2], r ^ 2, c)
         send(ref, ref, ds_.at[k], dr.at[k], r ^ 1, c)
 
-    pass_on(0)
-    round_x(2)
-    round_x(3)
-    pass_on(1)
-
-    for j in range(4):
+    def round_on(j):
         came, group, to = ((1, ql, right), (0, qr, left))[j % 2]
         ref = piece(j, group)
         arrived(ref, xr.at[came, j])
         send(ref, ref, xs.at[2, j], xr.at[2, j], r, to)
+
+    pass_on(0)
+    round_on(0)
+    round_on(1)
+    round_x(2)
+    round_x(3)
+    pass_on(1)
 
     def from_core(k, rs, hs):
         arrived(cotg.at[rows_of(rs), half_of(hs)], dr.at[k])
@@ -241,33 +243,41 @@
         return carry
 
     lax.fori_loop(0, 4, all_first, 0)
-    pass_on(2)
-    from_core(0, r ^ 1, o)
-    from_core(2, r ^ 3, o)
+    round_on(2)
+    round_on(3)
 
     load_m.wait()
     sq[...] = jnp.zeros_like(sq)
 
-    def grad_step(group, first=False, last=False):
+    def grad_step(group, which, first=False, last=False):
         def tile(rows):
-            part = jnp.dot(tokg[rows, rows_of(group)], cotg[rows_of(group), :], preferred_element_type=F32)
-            old = newm_ref[rows, :]
+            part = jnp.dot(
+                tokg[rows, rows_of(group)], cotg[rows_of(group), half_of(which)], preferred_element_type=F32
+            )
+            old = newm_ref[rows, half_of(which)]
             new = (BETA * old if first else old) + part
-            newm_ref[rows, :] = new
+            newm_ref[rows, half_of(which)] = new
             if last:
-                sq[...] += jnp.sum((new * new).reshape(-1, 8, BC), axis=0)
+                sq[...] += jnp.sum((new * new).reshape(-1, 8, HALF), axis=0)
 
         tiles(tile)
 
-    grad_step(q0, first=True)
+    pass_on(2)
+    grad_step(q0, h, first=True)
     for j in range(4):
         came, group = ((0, qr), (1, ql))[j % 2]
         arrived(piece(j, group), xr.at[came, j])
-    grad_step(ql)
-    grad_step(qr)
+    grad_step(ql, h)
+    grad_step(qr, h)
+    from_core(0, r ^ 1, o)
+    from_core(2, r ^ 3, o)
+    grad_step(q0, o, first=True)
+    grad_step(ql, o)
+    grad_step(qr, o)
     for j in range(4):
         arrived(piece(j, q2), xr.at[2, j])
-    grad_step(q2, last=True)
+    grad_step(q2, h, last=True)
+    grad_step(q2, o, last=True)
 
     MID = BR // 2
     top, low = pl.ds(0, MID), pl.ds(MID, MID)
@@ -373,21 +383,31 @@
         ).astype(BF16)
         return carry
 
-    def pieces_of(which):
-        return pl.ds(pl.multiple_of(which * MID, MID), MID)
-
-    def spread_sums(k, rd, cd):
-        part = sb.at[pl.ds(pl.multiple_of((2 * yb + k) * FEAT, FEAT), FEAT), :]
-        return (
-            remote(part, ib.at[zl], s2s.at[k], s2r.at[zl], rd, cd),
-            pltpu.make_async_copy(part, ib.at[zl], s2r.at[zl]),
+    def sum_rows(at):
+        return sb.at[pl.ds(pl.multiple_of((at % 4) * FEAT, FEAT), FEAT), :]
+
+    def pair_send():
+        for k in range(2):
+            send(sum_rows(2 * yb + 2 + k), sp.at[k], s2s.at[2 + k], s2r.at[2 + k], r, c ^ 2)
+
+    def pair_sum(k):
+        arrived(sp.at[k], s2r.at[2 + k])
+
+        def add(i, carry):
+            part = pl.ds(pl.multiple_of(i * 64, 64), 64)
+            here = pl.ds(pl.multiple_of((2 * yb + k) * FEAT + i * 64, 64), 64)
+            sb[here, :] = (sb[here, :].astype(F32) + sp[k, part, :].astype(F32)).astype(BF16)
+            return carry
+
+        lax.fori_loop(0, FEAT // 64, add, 0)
+        rd, cd, own = spread_sources()[k]
+        return send_spread(
+            [(rd, cd, own)],
+            lambda _, rd, cd: (
+                remote(sum_rows(2 * yb + k), ib.at[zl], s2s.at[k], s2r.at[zl], rd, cd),
+                pltpu.make_async_copy(sum_rows(2 * yb + k), ib.at[zl], s2r.at[zl]),
+            ),
         )
-
-    def pair_sum(i, carry):
-        part = pl.ds(pl.multiple_of(i * 64, 64), 64)
-        here = pl.ds(pl.multiple_of(yb * MID + i * 64, 64), 64)
-        sb[here, :] = (sb[here, :].astype(F32) + sp[part, :].astype(F32)).astype(BF16)
-        return carry
 
     def relay(k, t):
         ref = ub.at[2 * froms[k][0] + froms[k][1], chunk(t), :]
@@ -401,7 +421,7 @@
         arrived(ub.at[2 * rs + hs, chunk(t), :], vr.at[k, t])
         update_rows(rs, hs, t)
 
-    for t in range(CH):
+    for t in range(2):
         relay(0, t)
         relay(1, t)
         core_rows(3, t)
@@ -412,26 +432,31 @@
         arrived(ref.at[3 - j], pr.at[i, j])
 
     lax.fori_loop(0, MID // 64, total, 0)
+    core_rows(3, 2)
+    pair_send()
+    relay(0, 2)
+    relay(1, 2)
     for t in range(CH):
         core_rows(0, t)
-    send(sb.at[pieces_of(1 - yb), :], sp, s2s.at[2], s2r.at[2], r, c ^ 2)
-    for t in range(CH):
-        core_rows(1, t)
-    for t in range(CH):
-        relay(2, t)
-        update_rows(*froms[2], t)
-        if t == 0:
-            arrived(sp, s2r.at[2])
-            lax.fori_loop(0, MID // 64, pair_sum, 0)
-            core_rows(2, 0)
-            spreads += send_spread(spread_sources(), spread_sums)
-        elif t == 1:
-            core_rows(2, 1)
-        else:
-            for j in range(2):
-                arrived(ib.at[j], s2r.at[j])
-            ig_ref[...] = (ib[0].astype(F32) + ib[1].astype(F32)).astype(BF16)
-            core_rows(2, 2)
+        if t < 2:
+            core_rows(1, t)
+    spreads += pair_sum(0)
+    update_rows(*froms[0], 2)
+    update_rows(*froms[1], 2)
+    relay(2, 0)
+    spreads += pair_sum(1)
+    core_rows(1, 2)
+    update_rows(*froms[2], 0)
+    core_rows(2, 0)
+    relay(2, 1)
+    update_rows(*froms[2], 1)
+    core_rows(2, 1)
+    relay(2, 2)
+    update_rows(*froms[2], 2)
+    for j in range(2):
+        arrived(ib.at[j], s2r.at[j])
+    ig_ref[...] = (ib[0].astype(F32) + ib[1].astype(F32)).astype(BF16)
+    core_rows(2, 2)
 
     for cp, own in spreads:
         @pl.when(jnp.logical_not(own))
@@ -462,19 +487,19 @@
             pltpu.VMEM((BR, BC), BF16),
             pltpu.VMEM((BR, 4 * TOK), F32),
             pltpu.VMEM((BR, 4 * TOK), BF16),
-            pltpu.VMEM((8, BC), F32),
+            pltpu.VMEM((8, HALF), F32),
             pltpu.VMEM((2, BR, BR), BF16),
             pltpu.VMEM((BR, BC), BF16),
             pltpu.VMEM((3, BR // 2, TOK), BF16),
             pltpu.VMEM((3, BR // 2, TOK), BF16),
             pltpu.VMEM((BR, TOK), BF16),
-            pltpu.VMEM((BR // 2, TOK), BF16),
+            pltpu.VMEM((2, FEAT, TOK), BF16),
             pltpu.VMEM((2, FEAT, TOK), BF16),
             pltpu.VMEM((8, BR, HALF), BF16),
             dma((4,)), dma((4,)), dma((3, 4)), dma((3, 4)), dma((3,)), dma((3,)),
             dma((4,)), dma((4,)), dma((1,)), dma((1,)), dma((5,)),
             dma((2, 3)), dma((2, 3)), dma((3, CH)), dma((3, CH)), dma((4, CH)), dma((4, CH)),
-            dma((3,)), dma((3,)),
+            dma((4,)), dma((4,)),
         ],
         compiler_params=pltpu.CompilerParams(
             collective_id=0, has_side_effects=True, vmem_limit_bytes=40_000_000

time: 125 us -> 122 us (0.976)
  the two profiles are of different devices: /device:TPU:37 before, /device:TPU:0 now
where the time goes in v5:
time: 122 us
  Pallas kernels  122 us (100%)
    pallas_call x1, Pallas kernels, step_call(): pl.pallas_call(step_kernel, out_shape=(jax.ShapeDtypeStruct((BR, BC), F32...  117 us
    pallas_call x1, Pallas kernels, write_call(): pl.pallas_call(write_kernel, out_shape=(jax.ShapeDtypeStruct(newm.shape,...  4.73 us

profile of v5, /device:TPU:0, one launch (start us, length us, event | category | flops | bytes accessed | tf_op | source)
XLA Modules:
  0.0 122.4 jit_solution(8387865867863315721)
XLA Ops:
  0.6 117.0 %step.1 = (f32[768,1024]{1,0:T(8,128)S(1)}, bf16[768,1024]{1,0:T(8,128)(2,1)S(1)}, bf16[192,512]{1,0:T(8,128)(2,1)S(1)}, bf16[6144,512]{1,0:T(8,128)(2,1)S(1)}) custom-call(bf16[192,512]{1,0:T(8,128)(2,1)} %bitcast.8, bf16[512,512]{1,0:T(8,128)(2,1)} %cot_ref.1, bf16[6144,512]{1,0:T(8,128)(2,1)} %w_ref.1, f32[768,1024]{1,0:T(8,128)} %bitcast.5), custom_call_target="tpu_custom_call" | custom-call | flops 14000000000 | bytes 20000000 | tf_op jit(solution)/shard_map/step/pallas_call | solution.py:473
  117.7 4.7 %write_out.1 = (f32[768,1024]{1,0:T(8,128)}, f32[768,1024]{1,0:T(8,128)}, bf16[192,512]{1,0:T(8,128)(2,1)}, bf16[6144,512]{1,0:T(8,128)(2,1)}) custom-call(f32[768,1024]{1,0:T(8,128)S(1)} %get-tuple-element.12.newm_ref, bf16[768,1024]{1,0:T(8,128)(2,1)S(1)} %get-tuple-element.13.x_ref, bf16[192,512]{1,0:T(8,128)(2,1)S(1)} %get-tuple-element.14.ig_ref, ...), custom_call_target="tpu_custom_call" | custom-call | flops 1000000 | bytes 13000000 | tf_op jit(solution)/shard_map/write_out/pallas_call | solution.py:532

commit v6 on v5

--- a/solution.py
+++ b/solution.py
@@ -311,9 +311,11 @@
     def start_sums():
         arrived(wcat.at[:, half_of(o)], wr.at[0])
         terms_half(o, q2, False)
-        terms_half(o, qr, False)
         send(terms.at[top, rows_of(q2)], fl.at[0], ps.at[0, 0], pr.at[0, 0], r, right)
         send(terms.at[low, rows_of(q2)], fr.at[0], ps.at[1, 0], pr.at[1, 0], r, left)
+
+    def other_sums():
+        terms_half(o, qr, False)
         terms_half(o, ql, False)
         send(terms.at[low, rows_of(qr)], fl.at[2], ps.at[0, 1], pr.at[0, 1], r, right)
         terms_half(o, q0, False)
@@ -368,6 +370,7 @@
             send_update(2)
         src, dst = dst, src
 
+    other_sums()
     update_rows(r, h, 1, own=True)
     update_rows(r, h, 2, own=True)
     join_both()

time: 122 us -> 119 us (0.975)
  Pallas kernels: 122 us -> 119 us
    pallas_call x1, Pallas kernels: 117 us -> 114 us  [step_call(): pl.pallas_call(step_kernel, out_shape=(jax.ShapeDtypeStruct((BR, BC), F32...]
where the time goes in v6:
time: 119 us
  Pallas kernels  119 us (100%)
    pallas_call x1, Pallas kernels, step_call(): pl.pallas_call(step_kernel, out_shape=(jax.ShapeDtypeStruct((BR, BC), F32...  114 us
    pallas_call x1, Pallas kernels, write_call(): pl.pallas_call(write_kernel, out_shape=(jax.ShapeDtypeStruct(newm.shape,...  4.73 us

profile of v6, /device:TPU:0, one launch (start us, length us, event | category | flops | bytes accessed | tf_op | source)
XLA Modules:
  0.0 119.2 jit_solution(12035777363772042071)
XLA Ops:
  0.6 113.9 %step.1 = (f32[768,1024]{1,0:T(8,128)S(1)}, bf16[768,1024]{1,0:T(8,128)(2,1)S(1)}, bf16[192,512]{1,0:T(8,128)(2,1)S(1)}, bf16[6144,512]{1,0:T(8,128)(2,1)S(1)}) custom-call(bf16[192,512]{1,0:T(8,128)(2,1)} %bitcast.8, bf16[512,512]{1,0:T(8,128)(2,1)} %cot_ref.1, bf16[6144,512]{1,0:T(8,128)(2,1)} %w_ref.1, f32[768,1024]{1,0:T(8,128)} %bitcast.5), custom_call_target="tpu_custom_call" | custom-call | flops 14000000000 | bytes 20000000 | tf_op jit(solution)/shard_map/step/pallas_call | solution.py:476
  114.5 4.7 %write_out.1 = (f32[768,1024]{1,0:T(8,128)}, f32[768,1024]{1,0:T(8,128)}, bf16[192,512]{1,0:T(8,128)(2,1)}, bf16[6144,512]{1,0:T(8,128)(2,1)}) custom-call(f32[768,1024]{1,0:T(8,128)S(1)} %get-tuple-element.12.newm_ref, bf16[768,1024]{1,0:T(8,128)(2,1)S(1)} %get-tuple-element.13.x_ref, bf16[192,512]{1,0:T(8,128)(2,1)S(1)} %get-tuple-element.14.ig_ref, ...), custom_call_target="tpu_custom_call" | custom-call | flops 1000000 | bytes 13000000 | tf_op jit(solution)/shard_map/write_out/pallas_call | solution.py:535
